TPU v7x, 8 devices: a whole 2x2x1 slice. The times are simulated.
8 devices in a mesh: fsdp: 4 (over z, y, x), model: 2 (over core).
Axes of the slice: x: 2, y: 2, z: 1, core: 2. Of those that a mesh axis runs over, the one named last changes fastest.
Arguments:
- x_in: bfloat16 [16, 1024, 1536], P('fsdp', 'model')
- grad_out: bfloat16 [16, 1024, 1536], P('fsdp', 'model')
- gain_attn: float32 [1536], replicated
- gain_mlp: float32 [1536], replicated
- w_qkv: bfloat16 [1536, 2048], P('fsdp', 'model')
- w_out: bfloat16 [1536, 1536], P('model', 'fsdp')
- w_gate: bfloat16 [1536, 8960], P('fsdp', 'model')
- w_up: bfloat16 [1536, 8960], P('fsdp', 'model')
- w_down: bfloat16 [8960, 1536], P('model', 'fsdp')
- rope_cos: float32 [1024, 64], replicated
- rope_sin: float32 [1024, 64], replicated
Outputs:
- output 1: bfloat16 [16, 1024, 1536], P('fsdp', 'model')
- output 2: bfloat16 [16, 1024, 1536], P('fsdp', 'model')
- output 3: float32 [1536], replicated
- output 4: float32 [1536], replicated
- output 5: float32 [1536, 2048], P('fsdp', 'model')
- output 6: float32 [1536, 1536], P('model', 'fsdp')
- output 7: float32 [1536, 8960], P('fsdp', 'model')
- output 8: float32 [1536, 8960], P('fsdp', 'model')
- output 9: float32 [8960, 1536], P('model', 'fsdp')
All inputs are finite; a program needn't handle non-finite values.
Results may differ from a plain program's by a relative error of at most 0.0157642.
Values are sent between devices in bfloat16 or wider.
A program may use at most 1 GiB of HBM per device.

v0:
```python
import jax
import jax.numpy as jnp
from jax import lax
from jax.sharding import PartitionSpec as P

NORM_EPS = 1e-5


def rms_scale(x_f32, gain):
    inv_rms = lax.rsqrt(jnp.mean(x_f32 * x_f32, axis=-1, keepdims=True) + NORM_EPS)
    return x_f32 * inv_rms * gain


def rotate(tensor, cos_t, sin_t):
    half = tensor.shape[-1] // 2
    first = tensor[..., :half]
    second = tensor[..., half:]
    return jnp.concatenate([first * cos_t - second * sin_t, second * cos_t + first * sin_t], axis=-1)


def rotate_back(cotangent, cos_t, sin_t):
    half = cotangent.shape[-1] // 2
    first = cotangent[..., :half]
    second = cotangent[..., half:]
    return jnp.concatenate([first * cos_t + second * sin_t, second * cos_t - first * sin_t], axis=-1)


def solution(mesh):
    fsdp_size = mesh.shape['fsdp']
    act_spec = P('fsdp', 'model', None)
    rows_spec = P('fsdp', 'model')
    cols_spec = P('model', 'fsdp')

    def gather_rows(w_shard):
        return lax.all_gather(w_shard, 'fsdp', axis=0, tiled=True)

    def gather_cols(w_shard):
        return lax.all_gather(w_shard, 'fsdp', axis=1, tiled=True)

    def gather_seq(tensor):
        return lax.all_gather(tensor, 'model', axis=1, tiled=True)

    def scatter_seq(tensor):
        return lax.psum_scatter(tensor, 'model', scatter_dimension=1, tiled=True)

    def device_fn(x_loc, dy_loc, gain_attn, gain_mlp, wqkv_sh, wout_sh, wgate_sh, wup_sh, wdown_sh, rope_cos, rope_sin):
        head_dim = 2 * rope_cos.shape[1]
        seq_full = rope_cos.shape[0]
        local_heads = wout_sh.shape[0] // head_dim
        local_kv = (wqkv_sh.shape[1] // head_dim - local_heads) // 2
        group_size = local_heads // local_kv
        micro_rows = x_loc.shape[0] // 2
        scale = head_dim ** -0.5
        pos_ids = jnp.arange(seq_full)
        causal = pos_ids[:, None] >= pos_ids[None, :]
        cos_q = rope_cos[:, None, None, :]
        sin_q = rope_sin[:, None, None, :]
        cos_k = rope_cos[:, None, :]
        sin_k = rope_sin[:, None, :]

        def micro_step(x_mb, dy_mb, accum):
            acc_gattn, acc_gmlp, acc_qkv, acc_out, acc_gate, acc_up, acc_down = accum
            x_f32 = x_mb.astype(jnp.float32)
            h_attn_f, norm_back_attn = jax.vjp(rms_scale, x_f32, gain_attn)
            h_attn = gather_seq(h_attn_f.astype(jnp.bfloat16))
            w_qkv = gather_rows(wqkv_sh)
            qkv = jnp.einsum('bsd,dc->bsc', h_attn, w_qkv, preferred_element_type=jnp.float32)
            qkv = qkv.reshape(micro_rows, seq_full, local_kv, group_size + 2, head_dim)
            query = rotate(qkv[:, :, :, :group_size], cos_q, sin_q).astype(jnp.bfloat16)
            key_rot = rotate(qkv[:, :, :, group_size], cos_k, sin_k).astype(jnp.bfloat16)
            value = qkv[:, :, :, group_size + 1].astype(jnp.bfloat16)
            scores = jnp.einsum('bqkgd,btkd->bkgqt', query, key_rot, preferred_element_type=jnp.float32) * scale
            attn_prob = jax.nn.softmax(jnp.where(causal, scores, -1e30), axis=-1)
            prob_bf = attn_prob.astype(jnp.bfloat16)
            attn = jnp.einsum('bkgqt,btkd->bqkgd', prob_bf, value, preferred_element_type=jnp.float32)
            attn_flat = attn.astype(jnp.bfloat16).reshape(micro_rows, seq_full, local_heads * head_dim)
            w_out = gather_cols(wout_sh)
            attn_red = scatter_seq(jnp.einsum('bsh,hd->bsd', attn_flat, w_out, preferred_element_type=jnp.float32))
            mid_f32 = (x_f32 + attn_red.astype(jnp.bfloat16).astype(jnp.float32)).astype(jnp.bfloat16).astype(jnp.float32)
            h_mlp_f, norm_back_mlp = jax.vjp(rms_scale, mid_f32, gain_mlp)
            h_mlp = gather_seq(h_mlp_f.astype(jnp.bfloat16))
            w_gate = gather_rows(wgate_sh)
            w_up = gather_rows(wup_sh)
            gate = jnp.einsum('bsd,df->bsf', h_mlp, w_gate, preferred_element_type=jnp.float32)
            up_proj = jnp.einsum('bsd,df->bsf', h_mlp, w_up, preferred_element_type=jnp.float32)
            sig_gate = jax.nn.sigmoid(gate)
            silu_gate = gate * sig_gate
            gated_act = (silu_gate * up_proj).astype(jnp.bfloat16)
            w_down = gather_cols(wdown_sh)
            mlp_red = scatter_seq(jnp.einsum('bsf,fd->bsd', gated_act, w_down, preferred_element_type=jnp.float32))
            y_mb = (mid_f32 + mlp_red.astype(jnp.bfloat16).astype(jnp.float32)).astype(jnp.bfloat16)

            dy_full = gather_seq(dy_mb)
            w_down_b = gather_cols(wdown_sh)
            d_act = jnp.einsum('bsd,fd->bsf', dy_full, w_down_b, preferred_element_type=jnp.float32).astype(jnp.bfloat16).astype(jnp.float32)
            acc_down = acc_down + jnp.einsum('bsf,bsd->fd', gated_act, dy_full, preferred_element_type=jnp.float32)
            d_gate = (d_act * up_proj * sig_gate * (1.0 + gate * (1.0 - sig_gate))).astype(jnp.bfloat16)
            d_up = (d_act * silu_gate).astype(jnp.bfloat16)
            w_gate_b = gather_rows(wgate_sh)
            w_up_b = gather_rows(wup_sh)
            dh_mlp = scatter_seq(jnp.einsum('bsf,df->bsd', d_gate, w_gate_b, preferred_element_type=jnp.float32)
                                 + jnp.einsum('bsf,df->bsd', d_up, w_up_b, preferred_element_type=jnp.float32))
            acc_gate = acc_gate + jnp.einsum('bsd,bsf->df', h_mlp, d_gate, preferred_element_type=jnp.float32)
            acc_up = acc_up + jnp.einsum('bsd,bsf->df', h_mlp, d_up, preferred_element_type=jnp.float32)
            d_mid_norm, d_gain_mlp = norm_back_mlp(dh_mlp.astype(jnp.bfloat16).astype(jnp.float32))
            d_mid = (dy_mb.astype(jnp.float32) + d_mid_norm).astype(jnp.bfloat16)

            d_mid_full = gather_seq(d_mid)
            w_out_b = gather_cols(wout_sh)
            d_attn = jnp.einsum('bsd,hd->bsh', d_mid_full, w_out_b, preferred_element_type=jnp.float32).astype(jnp.bfloat16)
            acc_out = acc_out + jnp.einsum('bsh,bsd->hd', attn_flat, d_mid_full, preferred_element_type=jnp.float32)
            d_attn = d_attn.reshape(micro_rows, seq_full, local_kv, group_size, head_dim)
            d_prob = jnp.einsum('bqkgd,btkd->bkgqt', d_attn, value, preferred_element_type=jnp.float32)
            d_value = jnp.einsum('bkgqt,bqkgd->btkd', prob_bf, d_attn, preferred_element_type=jnp.float32)
            row_dot = jnp.sum(d_prob * attn_prob, axis=-1, keepdims=True)
            d_scores = (attn_prob * (d_prob - row_dot) * scale).astype(jnp.bfloat16)
            d_query = jnp.einsum('bkgqt,btkd->bqkgd', d_scores, key_rot, preferred_element_type=jnp.float32)
            d_key = jnp.einsum('bkgqt,bqkgd->btkd', d_scores, query, preferred_element_type=jnp.float32)
            d_qkv = jnp.concatenate([rotate_back(d_query, cos_q, sin_q),
                                     rotate_back(d_key, cos_k, sin_k)[:, :, :, None],
                                     d_value[:, :, :, None]], axis=3)
            d_qkv = d_qkv.astype(jnp.bfloat16).reshape(micro_rows, seq_full, -1)
            w_qkv_b = gather_rows(wqkv_sh)
            dh_attn = scatter_seq(jnp.einsum('bsc,dc->bsd', d_qkv, w_qkv_b, preferred_element_type=jnp.float32))
            acc_qkv = acc_qkv + jnp.einsum('bsd,bsc->dc', h_attn, d_qkv, preferred_element_type=jnp.float32)
            d_x_norm, d_gain_attn = norm_back_attn(dh_attn.astype(jnp.bfloat16).astype(jnp.float32))
            dx_mb = (d_mid.astype(jnp.float32) + d_x_norm).astype(jnp.bfloat16)
            new_accum = (acc_gattn + d_gain_attn, acc_gmlp + d_gain_mlp, acc_qkv, acc_out, acc_gate, acc_up, acc_down)
            return y_mb, dx_mb, new_accum

        accum = (jnp.zeros_like(gain_attn), jnp.zeros_like(gain_mlp),
                 jnp.zeros((wqkv_sh.shape[0] * fsdp_size, wqkv_sh.shape[1]), jnp.float32),
                 jnp.zeros((wout_sh.shape[0], wout_sh.shape[1] * fsdp_size), jnp.float32),
                 jnp.zeros((wgate_sh.shape[0] * fsdp_size, wgate_sh.shape[1]), jnp.float32),
                 jnp.zeros((wup_sh.shape[0] * fsdp_size, wup_sh.shape[1]), jnp.float32),
                 jnp.zeros((wdown_sh.shape[0], wdown_sh.shape[1] * fsdp_size), jnp.float32))
        y_parts = []
        dx_parts = []
        for micro_idx in range(2):
            lo_row = micro_idx * micro_rows
            y_mb, dx_mb, accum = micro_step(x_loc[lo_row:lo_row + micro_rows], dy_loc[lo_row:lo_row + micro_rows], accum)
            y_parts.append(y_mb)
            dx_parts.append(dx_mb)
        gain_grads = lax.psum((accum[0], accum[1]), ('fsdp', 'model'))
        return (jnp.concatenate(y_parts, axis=0), jnp.concatenate(dx_parts, axis=0), gain_grads[0], gain_grads[1],
                lax.psum_scatter(accum[2], 'fsdp', scatter_dimension=0, tiled=True),
                lax.psum_scatter(accum[3], 'fsdp', scatter_dimension=1, tiled=True),
                lax.psum_scatter(accum[4], 'fsdp', scatter_dimension=0, tiled=True),
                lax.psum_scatter(accum[5], 'fsdp', scatter_dimension=0, tiled=True),
                lax.psum_scatter(accum[6], 'fsdp', scatter_dimension=1, tiled=True))

    in_specs = (act_spec, act_spec, P(), P(), rows_spec, cols_spec, rows_spec, rows_spec, cols_spec, P(), P())
    out_specs = (act_spec, act_spec, P(), P(), rows_spec, cols_spec, rows_spec, rows_spec, cols_spec)
    return jax.shard_map(device_fn, mesh=mesh, in_specs=in_specs, out_specs=out_specs, check_vma=False)
```

profile of v0, /device:TPU:0, one launch (start us, length us, event | category | flops | bytes accessed | tf_op | source)
XLA Modules:
  0.0 2474.9 jit_solution(11574249283028735970)
XLA Ops:
  19.9 31.4 %all-gather.16.cloned.1.call-done = bf16[1536,1024]{0,1:T(8,128)(2,1)} async-done(((bf16[384,1024]{0,1:T(8,128)(2,1)}), bf16[1536,1024]{0,1:T(8,128)(2,1)}) %all-gather.16.cloned.1.call-update) | async-done | bytes 3145744 | tf_op jit(solution)/shard_map/all_gather | solution.py:35
  51.3 16.1 all-gather.28.cloned.1.call-done
  67.4 9.8 fusion.116
  84.7 9.8 fusion.118
  131.2 10.7 fusion.108
  142.0 24.6 fusion.12
  166.6 43.3 %fusion.9 = (f32[2,6,1024]{2,1,0:T(8,128)S(1)}, f32[2,6,1024]{2,1,0:T(8,128)S(1)}, f32[2,1024,1024,6]{2,1,3,0:T(8,128)}) fusion(f32[2,1024,1024,6]{2,1,3,0:T(8,128)} %get-tuple-element.81, f32[2,6,1024]{2,1,0:T(8,128)S(1)} %get-tuple-element.80, pred[1024,1024]{0,1:T(8,128)(4,1)S(1)} %iota_compare_fusion, bf16[2,1024,6,64]{3,1,2,0:T(8,128)(2,1)} %get-tuple-element.77, ...), kind=kOutput, calls=%fused_computation.21 | convolution fusion | flops 3316621312 | bytes 105529344 | tf_op jit(solution)/shard_map/bqkgd,btkd->bkgqt/dot_general | solution.py:72
  209.9 21.3 fusion.11
  231.2 23.8 fusion.137
  255.0 10.1 fusion.124
  265.2 29.1 %fusion.134 = bf16[2,128,6,1024]{3,1,2,0:T(8,128)(2,1)} fusion(f32[2,6,1024]{2,1,0:T(8,128)S(1)} %get-tuple-element.23, f32[2,6,1024]{2,1,0:T(8,128)S(1)} %get-tuple-element.80, f32[2,1024,1024,6]{2,1,3,0:T(8,128)} %get-tuple-element.81, pred[1024,1024]{0,1:T(8,128)(4,1)S(1)} %iota_compare_fusion, f32[2,1024,1,8,128]{1,4,3,0,2:T(8,128)} %bitcast.376), kind=kOutput, calls=%fused_computation.192 | convolution fusion | flops 3285712896 | bytes 55148544 | tf_op jit(solution)/shard_map/bkgqt,btkd->bqkgd/dot_general | solution.py:75
  294.3 10.0 fusion.126
  312.4 11.2 reduce-scatter.14.cloned.1.call-done
  323.6 9.7 fusion.93
  342.1 129.5 %all-gather.26.cloned.1.call-done = bf16[4480,1536]{1,0:T(8,128)(2,1)} async-done(((bf16[4480,384]{1,0:T(8,128)(2,1)}), bf16[4480,1536]{1,0:T(8,128)(2,1)}) %all-gather.26.cloned.1.call-update) | async-done | bytes 13762576 | tf_op jit(solution)/shard_map/all_gather | solution.py:38
  471.5 36.0 %fusion.60 = bf16[2,1024,4480]{2,1,0:T(8,128)(2,1)} fusion(bf16[2,1024,1536]{2,1,0:T(8,128)(2,1)} %all-gather.32.cloned.1.call-done, bf16[4480,1536]{1,0:T(8,128)(2,1)} %all-gather.26.cloned.1.call-done), kind=kOutput, calls=%fused_computation.79 | convolution fusion | flops 28194897920 | bytes 38404096 | tf_op jit(solution)/shard_map/bsd,fd->bsf/dot_general | solution.py:95
  507.6 92.4 %all-gather.22.cloned.1.call-done = bf16[1536,4480]{1,0:T(8,128)(2,1)} async-done(((bf16[384,4480]{1,0:T(8,128)(2,1)}), bf16[1536,4480]{1,0:T(8,128)(2,1)}) %all-gather.22.cloned.1.call-update) | async-done | bytes 13762576 | tf_op jit(solution)/shard_map/all_gather | solution.py:35
  600.0 15.4 all-gather.20.cloned.1.call-done
  615.4 36.5 %fusion.58 = f32[2,1024,4480]{2,1,0:T(8,128)} fusion(bf16[2,1024,1536]{2,1,0:T(8,128)(2,1)} %all-gather.20.cloned.1.call-done, bf16[1536,4480]{1,0:T(8,128)(2,1)} %all-gather.22.cloned.1.call-done), kind=kOutput, calls=%fused_computation.77 | convolution fusion | flops 28185722880 | bytes 56754176 | tf_op jit(solution)/shard_map/bsd,df->bsf/dot_general | solution.py:84
  651.9 93.1 %all-gather.24.cloned.1.call-done = bf16[1536,4480]{1,0:T(8,128)(2,1)} async-done(((bf16[384,4480]{1,0:T(8,128)(2,1)}), bf16[1536,4480]{1,0:T(8,128)(2,1)}) %all-gather.24.cloned.1.call-update) | async-done | bytes 13762576 | tf_op jit(solution)/shard_map/all_gather | solution.py:35
  745.0 53.5 %fusion.16 = (bf16[2,1024,4480]{2,1,0:T(8,128)(2,1)}, bf16[2,1024,4480]{2,1,0:T(8,128)(2,1)}, bf16[2,1024,4480]{2,1,0:T(8,128)(2,1)}) fusion(bf16[2,1024,4480]{2,1,0:T(8,128)(2,1)} %fusion.60, f32[2,1024,4480]{2,1,0:T(8,128)} %fusion.58, bf16[2,1024,1536]{2,1,0:T(8,128)(2,1)} %all-gather.20.cloned.1.call-done, ...), kind=kOutput, calls=%fused_computation.28 | convolution fusion | flops 28332523520 | bytes 130154496 | tf_op jit(solution)/shard_map/bsd,df->bsf/dot_general | solution.py:85
  798.5 37.9 %fusion.46 = f32[2,1024,1536]{2,1,0:T(8,128)} fusion(bf16[2,1024,4480]{2,1,0:T(8,128)(2,1)} %get-tuple-element.35, bf16[1536,4480]{1,0:T(8,128)(2,1)} %all-gather.24.cloned.1.call-done), kind=kOutput, calls=%fused_computation.65 | convolution fusion | flops 28185722880 | bytes 44695552 | tf_op jit(solution)/shard_map/bsf,df->bsd/dot_general | solution.py:102
  836.5 39.1 %fusion.102 = f32[2,1024,1536]{2,1,0:T(8,128)} fusion(f32[2,1024,1536]{2,1,0:T(8,128)} %fusion.46, bf16[2,1024,4480]{2,1,0:T(8,128)(2,1)} %get-tuple-element.31, bf16[1536,4480]{1,0:T(8,128)(2,1)} %all-gather.22.cloned.1.call-done), kind=kOutput, calls=%fused_computation.160 | convolution fusion | flops 28188868608 | bytes 57278464 | tf_op jit(solution)/shard_map/bsf,df->bsd/dot_general | solution.py:101
  876.4 17.3 reduce-scatter.22.cloned.1.call-done
  900.8 10.8 all-gather.36.cloned.1.call-done
  911.6 35.9 %fusion.63 = bf16[2,1024,4480]{2,1,0:T(8,128)(2,1)} fusion(bf16[2,1024,1536]{2,1,0:T(8,128)(2,1)} %all-gather.36.cloned.1.call-done, bf16[4480,1536]{1,0:T(8,128)(2,1)} %all-gather.26.cloned.1.call-done), kind=kOutput, calls=%fused_computation.80 | convolution fusion | flops 28194897920 | bytes 38404096 | tf_op jit(solution)/shard_map/bsd,fd->bsf/dot_general | solution.py:95
  947.5 36.5 %fusion.56 = f32[2,1024,4480]{2,1,0:T(8,128)} fusion(bf16[2,1024,1536]{2,1,0:T(8,128)(2,1)} %all-gather.30.cloned.1.call-done, bf16[1536,4480]{1,0:T(8,128)(2,1)} %all-gather.22.cloned.1.call-done), kind=kOutput, calls=%fused_computation.75 | convolution fusion | flops 28185722880 | bytes 56754176 | tf_op jit(solution)/shard_map/bsd,df->bsf/dot_general | solution.py:84
  984.1 53.5 %fusion.20 = (bf16[2,1024,4480]{2,1,0:T(8,128)(2,1)}, bf16[2,1024,4480]{2,1,0:T(8,128)(2,1)}, bf16[2,1024,4480]{2,1,0:T(8,128)(2,1)}) fusion(bf16[2,1024,4480]{2,1,0:T(8,128)(2,1)} %fusion.63, f32[2,1024,4480]{2,1,0:T(8,128)} %fusion.56, bf16[2,1024,1536]{2,1,0:T(8,128)(2,1)} %all-gather.30.cloned.1.call-done, ...), kind=kOutput, calls=%fused_computation.32 | convolution fusion | flops 28332523520 | bytes 130154496 | tf_op jit(solution)/shard_map/bsd,df->bsf/dot_general | solution.py:85
  1037.5 37.9 %fusion.44 = f32[2,1024,1536]{2,1,0:T(8,128)} fusion(bf16[2,1024,4480]{2,1,0:T(8,128)(2,1)} %get-tuple-element.36, bf16[1536,4480]{1,0:T(8,128)(2,1)} %all-gather.24.cloned.1.call-done), kind=kOutput, calls=%fused_computation.63 | convolution fusion | flops 28185722880 | bytes 44695552 | tf_op jit(solution)/shard_map/bsf,df->bsd/dot_general | solution.py:102
  1075.5 38.8 %fusion.105 = f32[2,1024,1536]{2,1,0:T(8,128)} fusion(f32[2,1024,1536]{2,1,0:T(8,128)} %fusion.44, bf16[2,1024,4480]{2,1,0:T(8,128)(2,1)} %get-tuple-element.33, bf16[1536,4480]{1,0:T(8,128)(2,1)} %all-gather.22.cloned.1.call-done), kind=kOutput, calls=%fused_computation.161 | convolution fusion | flops 28188868608 | bytes 57278464 | tf_op jit(solution)/shard_map/bsf,df->bsd/dot_general | solution.py:101
  1114.4 38.9 %fusion.42 = f32[2,1024,1536]{2,1,0:T(8,128)} fusion(bf16[2,1024,4480]{2,1,0:T(8,128)(2,1)} %get-tuple-element.32, bf16[4480,1536]{1,0:T(8,128)(2,1)} %all-gather.26.cloned.1.call-done), kind=kOutput, calls=%fused_computation.61 | convolution fusion | flops 28185722880 | bytes 44695552 | tf_op jit(solution)/shard_map/bsf,fd->bsd/dot_general | solution.py:90
  1153.3 38.9 %fusion.40 = f32[2,1024,1536]{2,1,0:T(8,128)} fusion(bf16[2,1024,4480]{2,1,0:T(8,128)(2,1)} %get-tuple-element.34, bf16[4480,1536]{1,0:T(8,128)(2,1)} %all-gather.26.cloned.1.call-done), kind=kOutput, calls=%fused_computation.59 | convolution fusion | flops 28185722880 | bytes 44695552 | tf_op jit(solution)/shard_map/bsf,fd->bsd/dot_general | solution.py:90
  1198.9 12.7 reduce-scatter.20.cloned.1.call-done
  1211.6 18.1 fusion.83
  1230.5 15.7 all-gather.38.cloned.1.call-done
  1246.3 9.2 fusion.131
  1255.5 21.6 fusion.166
  1277.1 21.1 fusion.155
  1298.2 9.2 fusion.128
  1307.4 67.9 %fusion.4 = (f32[2,6,1024]{2,1,0:T(8,128)S(1)}, f32[2,6,1024]{2,1,0:T(8,128)S(1)}, f32[2,1024,1024,6]{2,1,3,0:T(8,128)}) fusion(f32[2,6,1024]{2,1,0:T(8,128)S(1)} %copy-done.51, f32[2,6,1024]{2,1,0:T(8,128)S(1)} %copy-done.31, f32[2,1024,1024,6]{2,1,3,0:T(8,128)} %get-tuple-element.81, pred[1024,1024]{0,1:T(8,128)(4,1)S(1)} %copy-done.3, ...), kind=kOutput, calls=%fused_computation.10 | convolution fusion | flops 3372195840 | bytes 206340096 | tf_op jit(solution)/shard_map/bqkgd,btkd->bkgqt/dot_general | solution.py:113
  1375.3 81.1 %fusion.25 = (bf16[2,6,1024,1024]{2,3,1,0:T(8,128)(2,1)}, bf16[2,6,1024,1024]{2,3,1,0:T(8,128)(2,1)}) fusion(f32[2,1024,1024,6]{2,1,3,0:T(8,128)} %fusion.166, f32[2,6,1024]{2,1,0:T(8,128)S(1)} %get-tuple-element.22, f32[2,6,1024]{2,1,0:T(8,128)S(1)} %copy-done.35, f32[2,6,1024]{2,1,0:T(8,128)S(1)} %copy-done.33, f32[2,1024,1024,6]{2,1,3,0:T(8,128)} %get-tuple-element.82, ...), kind=kLoop, calls=%fused_computation.44 | loop fusion | flops 201326592 | bytes 253001728 | tf_op jit(solution)/shard_map/reshape.70
  1456.4 12.7 convolution_bitcast_fusion.3
  1469.2 17.9 convolution_bitcast_fusion.1
  1487.0 14.2 convolution_bitcast_fusion.2
  1501.3 17.5 convolution_bitcast_fusion
  1522.5 9.3 add_convert_fusion
  1542.5 12.7 fusion.112
  1556.7 26.1 %fusion.152 = bf16[2,1024,1,1,128]{4,1,3,0,2:T(8,128)(2,1)S(1)} fusion(bf16[2,1024,6,128]{1,3,2,0:T(8,128)(2,1)} %bitcast.389, f32[2,6,1024]{2,1,0:T(8,128)S(1)} %copy-done.51, f32[2,6,1024]{2,1,0:T(8,128)S(1)} %copy-done.31, f32[2,1024,1024,6]{2,1,3,0:T(8,128)} %get-tuple-element.81, pred[1024,1024]{0,1:T(8,128)(4,1)S(1)} %copy-done.3), kind=kOutput, calls=%fused_computation.200 | convolution fusion | flops 3284402176 | bytes 55148544 | tf_op jit(solution)/shard_map/bkgqt,bqkgd->btkd/dot_general | solution.py:114
  1594.2 11.5 fusion.114
  1614.4 11.6 bitcast_add_fusion.4
  1626.2 10.2 fusion.191
  1636.4 10.5 bitcast_add_fusion.3
  1647.0 37.2 %fusion.194 = f32[1536,4480,1]{1,0,2:T(8,128)} fusion(bf16[2,1024,1536]{2,1,0:T(8,128)(2,1)} %all-gather.20.cloned.1.call-done, bf16[2,1024,4480]{2,1,0:T(8,128)(2,1)} %get-tuple-element.35), kind=kOutput, calls=%fused_computation.250 | convolution fusion | flops 28185722880 | bytes 52166656 | tf_op jit(solution)/shard_map/bsd,bsf->df/dot_general | solution.py:104
  1684.3 42.0 %bitcast_add_fusion.1 = f32[1536,4480]{1,0:T(8,128)} fusion(f32[1536,4480,1]{1,0,2:T(8,128)} %fusion.194, bf16[2,1024,1536]{2,1,0:T(8,128)(2,1)} %all-gather.30.cloned.1.call-done, bf16[2,1024,4480]{2,1,0:T(8,128)(2,1)} %get-tuple-element.36), kind=kOutput, calls=%fused_computation.41 | convolution fusion | flops 28192604160 | bytes 79691776 | tf_op jit(solution)/shard_map/bsd,bsf->df/dot_general | solution.py:104
  1726.4 37.3 %fusion.195 = f32[4480,1536,1]{1,0,2:T(8,128)} fusion(bf16[2,1024,4480]{2,1,0:T(8,128)(2,1)} %get-tuple-element.32, bf16[2,1024,1536]{2,1,0:T(8,128)(2,1)} %all-gather.32.cloned.1.call-done), kind=kOutput, calls=%fused_computation.251 | convolution fusion | flops 28185722880 | bytes 52166656 | tf_op jit(solution)/shard_map/bsf,bsd->fd/dot_general | solution.py:96
  1763.7 38.2 %bitcast_add_fusion = f32[4480,1536]{1,0:T(8,128)} fusion(f32[4480,1536,1]{1,0,2:T(8,128)} %fusion.195, bf16[2,1024,4480]{2,1,0:T(8,128)(2,1)} %get-tuple-element.34, bf16[2,1024,1536]{2,1,0:T(8,128)(2,1)} %all-gather.36.cloned.1.call-done), kind=kOutput, calls=%fused_computation.40 | convolution fusion | flops 28192604160 | bytes 79691776 | tf_op jit(solution)/shard_map/bsf,bsd->fd/dot_general | solution.py:96
  1801.9 37.3 %fusion.193 = f32[1536,4480,1]{1,0,2:T(8,128)} fusion(bf16[2,1024,1536]{2,1,0:T(8,128)(2,1)} %all-gather.20.cloned.1.call-done, bf16[2,1024,4480]{2,1,0:T(8,128)(2,1)} %get-tuple-element.31), kind=kOutput, calls=%fused_computation.249 | convolution fusion | flops 28185722880 | bytes 52166656 | tf_op jit(solution)/shard_map/bsd,bsf->df/dot_general | solution.py:103
  1839.2 41.9 %bitcast_add_fusion.2 = f32[1536,4480]{1,0:T(8,128)} fusion(f32[1536,4480,1]{1,0,2:T(8,128)} %fusion.193, bf16[2,1024,1536]{2,1,0:T(8,128)(2,1)} %all-gather.30.cloned.1.call-done, bf16[2,1024,4480]{2,1,0:T(8,128)(2,1)} %get-tuple-element.33), kind=kOutput, calls=%fused_computation.42 | convolution fusion | flops 28192604160 | bytes 79691776 | tf_op jit(solution)/shard_map/bsd,bsf->df/dot_general | solution.py:103
  1888.6 9.4 fusion.79
  1898.0 23.0 all-reduce
  1921.0 9.8 fusion.85
  1934.0 56.4 %reduce-scatter.36.cloned.1.call-done = f32[384,4480]{1,0:T(8,128)} async-done(((f32[1536,4480]{1,0:T(8,128)}), f32[384,4480]{1,0:T(8,128)}) %reduce-scatter.36.cloned.1.call-update) | async-done | bytes 6881296 | tf_op jit(solution)/shard_map/reduce_scatter | solution.py:149
  1990.4 238.9 %reduce-scatter.38.cloned.1.call-done = f32[4480,384]{1,0:T(8,128)} async-done(((f32[4480,1536]{1,0:T(8,128)}), f32[4480,384]{1,0:T(8,128)}) %reduce-scatter.38.cloned.1.call-update) | async-done | bytes 6881296 | tf_op jit(solution)/shard_map/reduce_scatter | solution.py:150
  2229.4 238.8 %reduce-scatter.34.cloned.1.call-done = f32[384,4480]{1,0:T(8,128)} async-done(((f32[1536,4480]{1,0:T(8,128)}), f32[384,4480]{1,0:T(8,128)}) %reduce-scatter.34.cloned.1.call-update) | async-done | bytes 6881296 | tf_op jit(solution)/shard_map/reduce_scatter | solution.py:148
  (236 shorter events, 136.0 us)
Async XLA Ops:
  7.2 6.7 copy-start.39
  7.2 44.1 %all-gather.16.cloned.1.call-start = ((), (), s32[]{:S(2)}) async-start(), calls=%async_computation.14 | async-start | bytes 3932160 | tf_op jit(solution)/shard_map/all_gather | solution.py:35
  9.5 57.9 %all-gather.28.cloned.1.call-start = ((), (), s32[]{:S(2)}) async-start(), calls=%async_computation.22 | async-start | bytes 9437184 | tf_op jit(solution)/shard_map/all_gather | solution.py:41
  17.8 66.9 %all-gather.14.cloned.1.call-start = ((), (), s32[]{:S(2)}) async-start(), calls=%async_computation.13 | async-start | bytes 9437184 | tf_op jit(solution)/shard_map/all_gather | solution.py:41
  18.5 236.5 %all-gather.18.cloned.1.call-start = ((), (), s32[]{:S(2)}) async-start(), calls=%async_computation.15 | async-start | bytes 2949120 | tf_op jit(solution)/shard_map/all_gather | solution.py:38
  19.1 293.3 %reduce-scatter.18.cloned.1.call-start = ((), (), s32[]{:S(2)}) async-start(), calls=%async_computation.23 | async-start | bytes 18874368 | tf_op jit(solution)/shard_map/reduce_scatter | solution.py:44
  19.5 245.7 %copy-start.2 = (pred[1024,1024]{0,1:T(8,128)(4,1)}, pred[1024,1024]{0,1:T(8,128)(4,1)S(1)}, u32[]{:S(2)}) copy-start(pred[1024,1024]{0,1:T(8,128)(4,1)S(1)} %iota_compare_fusion) | copy-start | bytes 3145732
  19.7 111.5 %copy-start.9 = (f32[1024,64]{1,0:T(8,128)}, f32[1024,64]{1,0:T(8,128)S(1)}, u32[]{:S(2)}) copy-start(f32[1024,64]{1,0:T(8,128)S(1)} %copy.79) | copy-start | bytes 786436
  19.9 111.3 %copy-start.11 = (f32[1024,64]{1,0:T(8,128)}, f32[1024,64]{1,0:T(8,128)S(1)}, u32[]{:S(2)}) copy-start(f32[1024,64]{1,0:T(8,128)S(1)} %copy.80) | copy-start | bytes 786436
  131.2 10.7 copy-start.18
  131.2 10.7 copy-start.20
  141.9 24.7 copy-start.13
  141.9 24.7 copy-start.23
  141.9 24.6 copy-start.24
  166.6 98.6 %copy-start.30 = (f32[2,6,1024]{2,1,0:T(8,128)}, f32[2,6,1024]{2,1,0:T(8,128)S(1)}, u32[]{:S(2)}) copy-start(f32[2,6,1024]{2,1,0:T(8,128)S(1)} %get-tuple-element.80) | copy-start | bytes 147460
  209.9 21.3 copy-start.32
  209.9 55.3 %copy-start.50 = (f32[2,6,1024]{2,1,0:T(8,128)}, f32[2,6,1024]{2,1,0:T(8,128)S(1)}, u32[]{:S(2)}) copy-start(f32[2,6,1024]{2,1,0:T(8,128)S(1)} %get-tuple-element.23) | copy-start | bytes 147460
  231.2 23.8 copy-start.34
  265.1 58.4 %reduce-scatter.14.cloned.1.call-start = ((), (), s32[]{:S(2)}) async-start(), calls=%async_computation.16 | async-start | bytes 18874368 | tf_op jit(solution)/shard_map/reduce_scatter | solution.py:44
  304.4 37.6 %all-gather.32.cloned.1.call-start = ((), (), s32[]{:S(2)}) async-start(), calls=%async_computation.26 | async-start | bytes 9437184 | tf_op jit(solution)/shard_map/all_gather | solution.py:41
  310.8 160.7 %all-gather.26.cloned.1.call-start = ((), (), s32[]{:S(2)}) async-start(), calls=%async_computation.20 | async-start | bytes 17203200 | tf_op jit(solution)/shard_map/all_gather | solution.py:38
  311.6 288.4 %all-gather.22.cloned.1.call-start = ((), (), s32[]{:S(2)}) async-start(), calls=%async_computation.18 | async-start | bytes 17203200 | tf_op jit(solution)/shard_map/all_gather | solution.py:35
  312.3 22.6 copy-start.36
  312.3 303.0 %all-gather.20.cloned.1.call-start = ((), (), s32[]{:S(2)}) async-start(), calls=%async_computation.17 | async-start | bytes 9437184 | tf_op jit(solution)/shard_map/all_gather | solution.py:41
  337.4 407.6 %all-gather.24.cloned.1.call-start = ((), (), s32[]{:S(2)}) async-start(), calls=%async_computation.19 | async-start | bytes 17203200 | tf_op jit(solution)/shard_map/all_gather | solution.py:35
  338.1 555.6 %reduce-scatter.22.cloned.1.call-start = ((), (), s32[]{:S(2)}) async-start(), calls=%async_computation.27 | async-start | bytes 18874368 | tf_op jit(solution)/shard_map/reduce_scatter | solution.py:44
  875.5 18.2 copy-start.5
  875.5 18.2 copy-start.37
  875.5 18.2 copy-start.48
  875.6 36.0 %all-gather.36.cloned.1.call-start = ((), (), s32[]{:S(2)}) async-start(), calls=%async_computation.30 | async-start | bytes 9437184 | tf_op jit(solution)/shard_map/all_gather | solution.py:41
  876.3 71.2 %all-gather.30.cloned.1.call-start = ((), (), s32[]{:S(2)}) async-start(), calls=%async_computation.24 | async-start | bytes 9437184 | tf_op jit(solution)/shard_map/all_gather | solution.py:41
  876.4 24.3 copy-start.45
  900.8 292.2 %reduce-scatter.26.cloned.1.call-start = ((), (), s32[]{:S(2)}) async-start(), calls=%async_computation.31 | async-start | bytes 18874368 | tf_op jit(solution)/shard_map/reduce_scatter | solution.py:44
  1114.3 84.6 %reduce-scatter.16.cloned.1.call-start = ((), (), s32[]{:S(2)}) async-start(), calls=%async_computation.21 | async-start | bytes 18874368 | tf_op jit(solution)/shard_map/reduce_scatter | solution.py:44
  1153.3 58.3 %reduce-scatter.20.cloned.1.call-start = ((), (), s32[]{:S(2)}) async-start(), calls=%async_computation.25 | async-start | bytes 18874368 | tf_op jit(solution)/shard_map/reduce_scatter | solution.py:44
  1192.3 6.6 copy-start.53
  1192.3 19.3 copy-start.6
  1192.3 19.3 copy-start.49
  1192.3 53.9 %all-gather.38.cloned.1.call-start = ((), (), s32[]{:S(2)}) async-start(), calls=%async_computation.32 | async-start | bytes 9437184 | tf_op jit(solution)/shard_map/all_gather | solution.py:41
  1229.7 16.5 copy-start.64
  1229.7 68.4 %all-gather.34.cloned.1.call-start = ((), (), s32[]{:S(2)}) async-start(), calls=%async_computation.28 | async-start | bytes 9437184 | tf_op jit(solution)/shard_map/all_gather | solution.py:41
  1230.5 658.0 %reduce-scatter.28.cloned.1.call-start = ((), (), s32[]{:S(2)}) async-start(), calls=%async_computation.33 | async-start | bytes 18874368 | tf_op jit(solution)/shard_map/reduce_scatter | solution.py:44
  1255.5 21.6 copy-start.3
  1255.5 21.6 copy-start.33
  1255.5 21.6 copy-start.35
  1298.2 9.2 copy-start.31
  1298.2 9.2 copy-start.51
  1375.3 81.1 %copy-start.14 = (bf16[2,1024,6,64]{3,1,2,0:T(8,128)(2,1)S(1)}, bf16[2,1024,6,64]{3,1,2,0:T(8,128)(2,1)}, u32[]{:S(2)}) copy-start(bf16[2,1024,6,64]{3,1,2,0:T(8,128)(2,1)} %copy-done.13) | copy-start | bytes 4718596
  1456.4 12.8 copy-start.19
  1456.4 12.8 copy-start.21
  1501.3 17.5 copy-start.10
  1501.3 17.5 copy-start.12
  1522.5 9.3 copy-start.27
  1555.3 333.3 %reduce-scatter.24.cloned.1.call-start = ((), (), s32[]{:S(2)}) async-start(), calls=%async_computation.29 | async-start | bytes 18874368 | tf_op jit(solution)/shard_map/reduce_scatter | solution.py:44
  1605.7 8.8 copy-start.65
  1605.7 328.4 %reduce-scatter.32.cloned.1.call-start = ((), (), s32[]{:S(2)}) async-start(), calls=%async_computation.35 | async-start | bytes 5898240 | tf_op jit(solution)/shard_map/reduce_scatter | solution.py:147
  1626.1 307.9 %reduce-scatter.30.cloned.1.call-start = ((), (), s32[]{:S(2)}) async-start(), calls=%async_computation.34 | async-start | bytes 7864320 | tf_op jit(solution)/shard_map/reduce_scatter | solution.py:146
  1626.1 10.3 copy-start.22
  1647.0 343.5 %reduce-scatter.36.cloned.1.call-start = ((), (), s32[]{:S(2)}) async-start(), calls=%async_computation.37 | async-start | bytes 34406400 | tf_op jit(solution)/shard_map/reduce_scatter | solution.py:149
  1726.3 503.1 %reduce-scatter.38.cloned.1.call-start = ((), (), s32[]{:S(2)}) async-start(), calls=%async_computation.38 | async-start | bytes 34406400 | tf_op jit(solution)/shard_map/reduce_scatter | solution.py:150
  1801.8 666.3 %reduce-scatter.34.cloned.1.call-start = ((), (), s32[]{:S(2)}) async-start(), calls=%async_computation.36 | async-start | bytes 34406400 | tf_op jit(solution)/shard_map/reduce_scatter | solution.py:148
  1888.5 32.5 %copy-start.57 = (f32[2,512]{1,0:T(2,128)S(1)}, f32[2,512]{1,0:T(2,128)}, u32[]{:S(2)}) copy-start(f32[2,512]{1,0:T(2,128)} %copy-done.56) | copy-start | bytes 12292
  1888.5 32.5 %copy-start.59 = (f32[2,512]{1,0:T(2,128)S(1)}, f32[2,512]{1,0:T(2,128)}, u32[]{:S(2)}) copy-start(f32[2,512]{1,0:T(2,128)} %copy-done.58) | copy-start | bytes 12292
  1888.5 32.5 %copy-start.7 = (bf16[2,512,1536]{2,1,0:T(8,128)(2,1)S(1)}, bf16[2,512,1536]{2,1,0:T(8,128)(2,1)}, u32[]{:S(2)}) copy-start(bf16[2,512,1536]{2,1,0:T(8,128)(2,1)} %get-tuple-element.51) | copy-start | bytes 9437188
  (28 other events, 70.4 us)
Sparse Core Ops, SparseCore 0:
  10.3 40.9 all-gather.15
  53.4 13.9 all-gather.27
  69.5 15.1 all-gather.13
  86.3 32.8 all-gather.17
  265.3 19.1 reduce-scatter.17
  304.5 19.0 reduce-scatter.13
  325.7 16.3 all-gather.31
  343.8 127.6 all-gather.25
  473.3 126.6 all-gather.21
  601.3 13.9 all-gather.19
  617.1 127.8 all-gather.23
  875.7 17.9 reduce-scatter.21
  895.2 16.3 all-gather.35
  913.5 15.1 all-gather.29
  1114.5 19.1 reduce-scatter.25
  1153.4 19.1 reduce-scatter.15
  1192.4 19.1 reduce-scatter.19
  1229.9 16.3 all-gather.37
  1247.8 15.1 all-gather.33
  1555.4 19.1 reduce-scatter.27
  1605.8 19.2 reduce-scatter.23
  1628.6 53.9 reduce-scatter.31
  1686.0 64.4 reduce-scatter.29
  1754.0 236.4 reduce-scatter.35
  1994.0 235.2 reduce-scatter.37
  2232.8 235.2 reduce-scatter.33
where the time goes:
time: 2480 us; the launch traced here: 2470 us
  matrix products  1160 us (47%)
  waiting for transfers between devices  989 us (40%)
  other arithmetic  218 us (9%)
  local copies, waits for them, and re-layouts  68.4 us (3%)
    reduce_scatter x1, waiting for transfers between devices, device_fn(): lax.psum_scatter(accum[6], 'fsdp', scatter_dimension=1, tiled=True)  239 us
    reduce_scatter x1, waiting for transfers between devices, device_fn(): lax.psum_scatter(accum[4], 'fsdp', scatter_dimension=0, tiled=True)  239 us
    all_gather x3, waiting for transfers between devices, gather_rows(): return lax.all_gather(w_shard, 'fsdp', axis=0, tiled=True)  217 us
    all_gather x2, waiting for transfers between devices, gather_cols(): return lax.all_gather(w_shard, 'fsdp', axis=1, tiled=True)  129 us
    dot_general x2, matrix products, micro_step(): jnp.einsum('bsd,df->bsf', h_mlp, w_up, preferred_element_type=jnp.float32)  107 us
    another operation x3, other arithmetic  93.8 us
    dot_general x2, matrix products, micro_step(): jnp.einsum('bqkgd,btkd->bkgqt', d_attn, value, preferred_element_type=jnp...  89.5 us
    dot_general x2, matrix products, micro_step(): jnp.einsum('bsd,bsf->df', h_mlp, d_up, preferred_element_type=jnp.float32)  79.3 us
  transfers between devices with their start and end apart: 26, of which 16 were waited for; matrix products, arithmetic and copies ran while one was open for 34% of the time, Pallas kernels for 0%

commit v1 on v0

v1 whole, which is shorter than its diff:
```python
import functools

import jax
import jax.numpy as jnp
from jax import lax
from jax.experimental import pallas as pl
from jax.experimental.pallas import tpu as pltpu
from jax.sharding import PartitionSpec as P


NORM_EPS = 1e-5
NEG = -1e30
QB = 256


def rms_scale(x_f32, gain):
    inv_rms = lax.rsqrt(jnp.mean(x_f32 * x_f32, axis=-1, keepdims=True) + NORM_EPS)
    return x_f32 * inv_rms * gain


def nt(a, b):
    return lax.dot_general(a, b, (((1,), (1,)), ((), ())), preferred_element_type=jnp.float32)


def nn(a, b):
    return lax.dot_general(a, b, (((1,), (0,)), ((), ())), preferred_element_type=jnp.float32)


def tn(a, b):
    return lax.dot_general(a, b, (((0,), (0,)), ((), ())), preferred_element_type=jnp.float32)


def causal_mask():
    rows = lax.broadcasted_iota(jnp.int32, (QB, QB), 0)
    cols = lax.broadcasted_iota(jnp.int32, (QB, QB), 1)
    return rows >= cols


def softmax_chunks(q, k_ref, blk, scale, mask):
    lo = blk * QB
    s_diag = jnp.where(mask, nt(q, k_ref[lo:lo + QB, :]) * scale, NEG)
    top = jnp.max(s_diag, axis=-1, keepdims=True)
    if blk:
        s_off = nt(q, k_ref[:lo, :]) * scale
        top = jnp.maximum(top, jnp.max(s_off, axis=-1, keepdims=True))
        e_off = jnp.exp(s_off - top)
        e_diag = jnp.exp(s_diag - top)
        inv = 1.0 / (jnp.sum(e_off, axis=-1, keepdims=True) + jnp.sum(e_diag, axis=-1, keepdims=True))
        return e_off * inv, e_diag * inv
    e_diag = jnp.exp(s_diag - top)
    return None, e_diag * (1.0 / jnp.sum(e_diag, axis=-1, keepdims=True))


def attn_fwd_kernel(heads, seq, dim, idx_ref, qkv_ref, cos_ref, sin_ref, rot_ref, out_ref, k_scr, v_scr):
    half_rows = seq // 2
    first = idx_ref[0]
    where_half = (first, 1 - first)
    mask = causal_mask()
    scale = dim ** -0.5
    kcol, vcol = heads * dim, (heads + 1) * dim
    for half in range(2):
        st = where_half[half]
        rows = slice(half * half_rows, (half + 1) * half_rows)
        key = qkv_ref[st, 0, :, kcol:kcol + dim]
        key = (key * cos_ref[st] + pltpu.roll(key, dim // 2, 1) * sin_ref[st]).astype(jnp.bfloat16)
        val = qkv_ref[st, 0, :, vcol:vcol + dim].astype(jnp.bfloat16)
        k_scr[rows, :] = key
        v_scr[rows, :] = val
        rot_ref[st, 0, :, kcol:kcol + dim] = key
        rot_ref[st, 0, :, vcol:vcol + dim] = val

    @pl.loop(0, heads)
    def _(h):
        col = pl.ds(pl.multiple_of(h * dim, dim), dim)
        for blk in range(seq // QB):
            st = where_half[blk * QB // half_rows]
            r0 = blk * QB % half_rows
            rows = slice(r0, r0 + QB)
            q = qkv_ref[st, 0, rows, col]
            q = (q * cos_ref[st, rows, :] + pltpu.roll(q, dim // 2, 1) * sin_ref[st, rows, :]).astype(jnp.bfloat16)
            rot_ref[st, 0, rows, col] = q
            p_off, p_diag = softmax_chunks(q, k_scr, blk, scale, mask)
            lo = blk * QB
            o = nn(p_diag.astype(jnp.bfloat16), v_scr[lo:lo + QB, :])
            if blk:
                o = o + nn(p_off.astype(jnp.bfloat16), v_scr[:lo, :])
            out_ref[st, 0, rows, col] = o.astype(jnp.bfloat16)


def attn_bwd_kernel(heads, seq, dim, idx_ref, rot_ref, do_ref, cos_ref, sin_ref, dqkv_ref, k_scr, v_scr, dk_scr, dv_scr):
    half_rows = seq // 2
    first = idx_ref[0]
    where_half = (first, 1 - first)
    mask = causal_mask()
    scale = dim ** -0.5
    kcol, vcol = heads * dim, (heads + 1) * dim
    for half in range(2):
        st = where_half[half]
        rows = slice(half * half_rows, (half + 1) * half_rows)
        k_scr[rows, :] = rot_ref[st, 0, :, kcol:kcol + dim]
        v_scr[rows, :] = rot_ref[st, 0, :, vcol:vcol + dim]
    dk_scr[...] = jnp.zeros_like(dk_scr)
    dv_scr[...] = jnp.zeros_like(dv_scr)

    @pl.loop(0, heads)
    def _(h):
        col = pl.ds(pl.multiple_of(h * dim, dim), dim)
        for blk in range(seq // QB):
            st = where_half[blk * QB // half_rows]
            r0 = blk * QB % half_rows
            rows = slice(r0, r0 + QB)
            lo = blk * QB
            q = rot_ref[st, 0, rows, col]
            do = do_ref[st, 0, rows, col]
            p_off, p_diag = softmax_chunks(q, k_scr, blk, scale, mask)
            dp_diag = nt(do, v_scr[lo:lo + QB, :])
            row_dot = jnp.sum(dp_diag * p_diag, axis=-1, keepdims=True)
            if blk:
                dp_off = nt(do, v_scr[:lo, :])
                row_dot = row_dot + jnp.sum(dp_off * p_off, axis=-1, keepdims=True)
            ds_diag = (p_diag * (dp_diag - row_dot) * scale).astype(jnp.bfloat16)
            dq = nn(ds_diag, k_scr[lo:lo + QB, :])
            dk_scr[lo:lo + QB, :] += tn(ds_diag, q)
            dv_scr[lo:lo + QB, :] += tn(p_diag.astype(jnp.bfloat16), do)
            if blk:
                ds_off = (p_off * (dp_off - row_dot) * scale).astype(jnp.bfloat16)
                dq = dq + nn(ds_off, k_scr[:lo, :])
                dk_scr[:lo, :] += tn(ds_off, q)
                dv_scr[:lo, :] += tn(p_off.astype(jnp.bfloat16), do)
            dq = dq * cos_ref[st, rows, :] - pltpu.roll(dq, dim // 2, 1) * sin_ref[st, rows, :]
            dqkv_ref[st, 0, rows, col] = dq.astype(jnp.bfloat16)

    for half in range(2):
        st = where_half[half]
        rows = slice(half * half_rows, (half + 1) * half_rows)
        dk = dk_scr[rows, :]
        dk = dk * cos_ref[st] - pltpu.roll(dk, dim // 2, 1) * sin_ref[st]
        dqkv_ref[st, 0, :, kcol:kcol + dim] = dk.astype(jnp.bfloat16)
        dqkv_ref[st, 0, :, vcol:vcol + dim] = dv_scr[rows, :].astype(jnp.bfloat16)


def seq_block(rows, cols):
    return pl.BlockSpec((2, 1, rows, cols), lambda b, idx: (0, b, 0, 0))


def table_block(rows, dim):
    return pl.BlockSpec((2, rows, dim), lambda b, idx: (0, 0, 0))


def attn_fwd(idx, qkv, cos_t, sin_t, heads):
    _, batch, rows, cols = qkv.shape
    dim = cos_t.shape[-1]
    flops = batch * heads * rows * rows * dim * 10
    return pl.pallas_call(
        functools.partial(attn_fwd_kernel, heads, 2 * rows, dim),
        out_shape=(jax.ShapeDtypeStruct(qkv.shape, jnp.bfloat16),
                   jax.ShapeDtypeStruct((2, batch, rows, heads * dim), jnp.bfloat16)),
        grid_spec=pltpu.PrefetchScalarGridSpec(
            num_scalar_prefetch=1, grid=(batch,),
            in_specs=[seq_block(rows, cols), table_block(rows, dim), table_block(rows, dim)],
            out_specs=[seq_block(rows, cols), seq_block(rows, heads * dim)],
            scratch_shapes=[pltpu.VMEM((2 * rows, dim), jnp.bfloat16)] * 2),
        cost_estimate=pl.CostEstimate(flops=flops, bytes_accessed=qkv.size * 8, transcendentals=batch * heads * rows * rows * 2),
        compiler_params=pltpu.CompilerParams(dimension_semantics=("arbitrary",)),
        name="attn_fwd",
    )(idx, qkv, cos_t, sin_t)


def attn_bwd(idx, rot, d_attn, cos_t, sin_t, heads):
    _, batch, rows, cols = rot.shape
    dim = cos_t.shape[-1]
    flops = batch * heads * rows * rows * dim * 25
    return pl.pallas_call(
        functools.partial(attn_bwd_kernel, heads, 2 * rows, dim),
        out_shape=jax.ShapeDtypeStruct(rot.shape, jnp.bfloat16),
        grid_spec=pltpu.PrefetchScalarGridSpec(
            num_scalar_prefetch=1, grid=(batch,),
            in_specs=[seq_block(rows, cols), seq_block(rows, heads * dim), table_block(rows, dim), table_block(rows, dim)],
            out_specs=seq_block(rows, cols),
            scratch_shapes=[pltpu.VMEM((2 * rows, dim), jnp.bfloat16)] * 2 + [pltpu.VMEM((2 * rows, dim), jnp.float32)] * 2),
        cost_estimate=pl.CostEstimate(flops=flops, bytes_accessed=rot.size * 6, transcendentals=batch * heads * rows * rows * 2),
        compiler_params=pltpu.CompilerParams(dimension_semantics=("arbitrary",)),
        name="attn_bwd",
    )(idx, rot, d_attn, cos_t, sin_t)


def solution(mesh):
    act_spec = P('fsdp', 'model', None)
    rows_spec = P('fsdp', 'model')
    cols_spec = P('model', 'fsdp')
    swap = [(0, 1), (1, 0)]

    def gather_rows(w_shard):
        return lax.all_gather(w_shard, 'fsdp', axis=0, tiled=True)

    def gather_cols(w_shard):
        return lax.all_gather(w_shard, 'fsdp', axis=1, tiled=True)

    def scatter(tensor, dim):
        return lax.psum_scatter(tensor, 'fsdp', scatter_dimension=dim, tiled=True)

    def partner(tensor):
        return lax.ppermute(tensor, 'model', swap)

    def both(own):
        return jnp.stack([own, partner(own)])

    def dot(spec, left, right):
        return jnp.einsum(spec, left, right, preferred_element_type=jnp.float32)

    def device_fn(x_loc, dy_loc, gain_attn, gain_mlp, wqkv_sh, wout_sh, wgate_sh, wup_sh, wdown_sh, rope_cos, rope_sin):
        dim = 2 * rope_cos.shape[1]
        heads = wout_sh.shape[0] // dim
        half_rows = x_loc.shape[1]
        me = lax.axis_index('model')
        idx = jnp.reshape(me, (1,)).astype(jnp.int32)

        def table(first, second):
            full = jnp.concatenate([first, second], axis=-1).reshape(2, half_rows, dim)
            return jnp.where(me == 0, full, full[::-1])

        cos_t = table(rope_cos, rope_cos)
        sin_t = table(-rope_sin, rope_sin)

        w_qkv = gather_rows(wqkv_sh)
        w_out = gather_cols(wout_sh)

        x_f32 = x_loc.astype(jnp.float32)
        h_attn_f, norm_back_attn = jax.vjp(rms_scale, x_f32, gain_attn)
        h_own = h_attn_f.astype(jnp.bfloat16)
        wgate_sh, h_own = lax.optimization_barrier((wgate_sh, h_own))
        w_gate = gather_rows(wgate_sh)
        h_attn = both(h_own)
        dy = both(dy_loc)
        qkv = dot('tbsd,dc->tbsc', h_attn, w_qkv)
        wup_sh, qkv = lax.optimization_barrier((wup_sh, qkv))
        w_up = gather_rows(wup_sh)
        rot, attn = attn_fwd(idx, qkv, cos_t, sin_t, heads)
        wdown_sh, attn = lax.optimization_barrier((wdown_sh, attn))
        w_down = gather_cols(wdown_sh)
        out_other = partner(dot('bsh,hd->bsd', attn[1], w_out))
        attn_red = dot('bsh,hd->bsd', attn[0], w_out) + out_other
        mid_f32 = (x_f32 + attn_red.astype(jnp.bfloat16).astype(jnp.float32)).astype(jnp.bfloat16).astype(jnp.float32)
        h_mlp_f, norm_back_mlp = jax.vjp(rms_scale, mid_f32, gain_mlp)
        h_mlp = both(h_mlp_f.astype(jnp.bfloat16))

        gate = dot('tbsd,df->tbsf', h_mlp, w_gate)
        up_proj = dot('tbsd,df->tbsf', h_mlp, w_up)
        sig_gate = jax.nn.sigmoid(gate)
        silu_gate = gate * sig_gate
        gated_act = (silu_gate * up_proj).astype(jnp.bfloat16)
        full_down, dy = lax.optimization_barrier((dot('tbsf,tbsd->fd', gated_act, dy), dy))
        dw_down = scatter(full_down, 1)

        d_act = dot('tbsd,fd->tbsf', dy, w_down).astype(jnp.bfloat16).astype(jnp.float32)
        d_gate = (d_act * up_proj * sig_gate * (1.0 + gate * (1.0 - sig_gate))).astype(jnp.bfloat16)
        d_up = (d_act * silu_gate).astype(jnp.bfloat16)
        full_gate, h_mlp = lax.optimization_barrier((dot('tbsd,tbsf->df', h_mlp, d_gate), h_mlp))
        dw_gate = scatter(full_gate, 0)
        full_up, d_gate, d_up = lax.optimization_barrier((dot('tbsd,tbsf->df', h_mlp, d_up), d_gate, d_up))
        dw_up = scatter(full_up, 0)

        def dh_of(part):
            return (dot('bsf,df->bsd', d_gate[part], w_gate)
                    + dot('bsf,df->bsd', d_up[part], w_up))

        dh_other = partner(dh_of(1))
        dh_mlp = dh_of(0) + dh_other
        d_mid_norm, d_gain_mlp = norm_back_mlp(dh_mlp.astype(jnp.bfloat16).astype(jnp.float32))
        d_mid = (dy_loc.astype(jnp.float32) + d_mid_norm).astype(jnp.bfloat16)
        d_mid_full = both(d_mid)

        d_attn = dot('tbsd,hd->tbsh', d_mid_full, w_out).astype(jnp.bfloat16)
        d_qkv = attn_bwd(idx, rot, d_attn, cos_t, sin_t, heads)
        dw_out = scatter(dot('tbsh,tbsd->hd', attn, d_mid_full), 1)
        dw_qkv = scatter(dot('tbsd,tbsc->dc', h_attn, d_qkv), 0)
        dha_other = partner(dot('bsc,dc->bsd', d_qkv[1], w_qkv))
        dh_attn = dot('bsc,dc->bsd', d_qkv[0], w_qkv) + dha_other
        d_x_norm, d_gain_attn = norm_back_attn(dh_attn.astype(jnp.bfloat16).astype(jnp.float32))
        dx = (d_mid.astype(jnp.float32) + d_x_norm).astype(jnp.bfloat16)

        y_other = partner(dot('bsf,fd->bsd', gated_act[1], w_down))
        mlp_red = dot('bsf,fd->bsd', gated_act[0], w_down) + y_other
        y_loc = (mid_f32 + mlp_red.astype(jnp.bfloat16).astype(jnp.float32)).astype(jnp.bfloat16)

        gain_grads = lax.psum((d_gain_attn, d_gain_mlp), ('fsdp', 'model'))
        return (y_loc, dx, gain_grads[0], gain_grads[1], dw_qkv, dw_out, dw_gate, dw_up, dw_down)

    in_specs = (act_spec, act_spec, P(), P(), rows_spec, cols_spec, rows_spec, rows_spec, cols_spec, P(), P())
    out_specs = (act_spec, act_spec, P(), P(), rows_spec, cols_spec, rows_spec, rows_spec, cols_spec)

    return jax.shard_map(device_fn, mesh=mesh, in_specs=in_specs, out_specs=out_specs, check_vma=False)
```

time: 2480 us -> 1840 us (0.74)
  matrix products: 1160 us -> 808 us
  waiting for transfers between devices: 989 us -> 770 us
  other arithmetic: 218 us -> 57.4 us
  Pallas kernels: 0 us -> 153 us
  local copies, waits for them, and re-layouts: 68.4 us -> 8.44 us
    dot_general x42 -> x20, matrix products: 1160 us -> 808 us  [dot(): return jnp.einsum(spec, left, right, preferred_element_type=jnp.float32)]
    pallas_call x0 -> x2, Pallas kernels: none -> 153 us  [the longest x1 92.2 us: attn_bwd(): pl.pallas_call(functools.partial(attn_bwd_kernel, heads, 2 * rows, dim),...]
    all_gather x2, waiting for transfers between devices: 129 us -> 0.02 us  [gather_cols(): return lax.all_gather(w_shard, 'fsdp', axis=1, tiled=True)]
    all_gather x3, waiting for transfers between devices: 217 us -> 98.7 us  [gather_rows(): return lax.all_gather(w_shard, 'fsdp', axis=0, tiled=True)]
    another operation x3, other arithmetic: 93.8 us -> 21.4 us  [both(): return jnp.stack([own, partner(own)])]
    all_gather x8 -> x0, waiting for transfers between devices: 62.1 us -> none  [gather_seq(): return lax.all_gather(tensor, 'model', axis=1, tiled=True)]
    reduce_scatter x13 -> x5, waiting for transfers between devices: 575 us -> 632 us  [scatter(): return lax.psum_scatter(tensor, 'fsdp', scatter_dimension=dim, tiled=True)]
    reduce_sum x4 -> x0, other arithmetic: 43.6 us -> none  [the longest x3 22.3 us: rms_scale(): return x_f32 * inv_rms * gain]
  transfers between devices with their start and end apart: 26 -> 18, of which waited for: 16 -> 9; matrix products, arithmetic and copies ran while one was open for 34% -> 26% of each run, Pallas kernels for 0% -> 8%
where the time goes in v1:
time: 1840 us
  matrix products  808 us (44%)
  waiting for transfers between devices  770 us (42%)
  Pallas kernels  153 us (8%)
  other arithmetic  57.4 us (3%)
  blocking collectives  23.5 us (1%)
    dot_general x20, matrix products, dot(): return jnp.einsum(spec, left, right, preferred_element_type=jnp.float32)  808 us
    reduce_scatter x5, waiting for transfers between devices, scatter(): return lax.psum_scatter(tensor, 'fsdp', scatter_dimension=dim, tiled=True)  632 us
    all_gather x3, waiting for transfers between devices, gather_rows(): return lax.all_gather(w_shard, 'fsdp', axis=0, tiled=True)  98.7 us
    pallas_call x1, Pallas kernels, attn_bwd(): pl.pallas_call(functools.partial(attn_bwd_kernel, heads, 2 * rows, dim),...  92.2 us
    pallas_call x1, Pallas kernels, attn_fwd(): pl.pallas_call(functools.partial(attn_fwd_kernel, heads, 2 * rows, dim),...  60.5 us
  transfers between devices with their start and end apart: 18, of which 9 were waited for; matrix products, arithmetic and copies ran while one was open for 26% of the time, Pallas kernels for 8%

profile of v1, /device:TPU:0, one launch (start us, length us, event | category | flops | bytes accessed | tf_op | source)
XLA Modules:
  0.0 1838.9 jit_solution(15089594743321900481)
XLA Ops:
  7.2 0.7 all-gather.6.cloned.1.call-update
  7.9 0.0 all-gather.8.cloned.1.call-start
  8.0 0.7 all-gather.8.cloned.1.call-update
  8.7 0.0 all-gather.10.cloned.1.call-start
  8.7 4.1 fusion.57
  12.9 7.0 fusion.50
  19.9 0.6 all-gather.12.cloned.1.call-start
  20.5 0.9 collective-permute-start
  21.4 0.2 copy.21
  21.7 0.2 copy.20
  21.9 1.0 reverse_select_fusion
  22.9 28.0 %all-gather.6.cloned.1.call-done = bf16[1536,1024]{1,0:T(8,128)(2,1)} async-done(((bf16[384,1024]{1,0:T(8,128)(2,1)}), bf16[1536,1024]{1,0:T(8,128)(2,1)}) %all-gather.6.cloned.1.call-update) | async-done | bytes 3145744 | tf_op jit(solution)/shard_map/all_gather | solution.py:194
  50.9 20.5 %fusion.94.qkv_ref = f32[2,4,512,1024]{3,2,1,0:T(8,128)} fusion(bf16[1536,1024]{1,0:T(8,128)(2,1)} %all-gather.6.cloned.1.call-done, bf16[1,4,512,1536]{3,2,1,0:T(8,128)(2,1)} %bitcast.2, bf16[1,4,512,1536]{3,2,1,0:T(8,128)(2,1)} %bitcast.152), kind=kOutput, calls=%fused_computation.104 | convolution fusion | flops 12891193344 | bytes 32505856 | tf_op jit(solution)/shard_map/tbsd,dc->tbsc/dot_general | solution.py:209
  71.4 60.5 %attn_fwd.1 = (bf16[2,4,512,1024]{3,2,1,0:T(8,128)(2,1)}, bf16[2,4,512,768]{3,2,1,0:T(8,128)(2,1)}) custom-call(s32[1]{0:T(128)} %bitcast.idx_ref, f32[2,4,512,1024]{3,2,1,0:T(8,128)} %fusion.94.qkv_ref, f32[2,512,128]{2,1,0:T(8,128)} %get-tuple-element.54.cos_ref, f32[2,512,128]{2,1,0:T(8,128)} %get-tuple-element.53.sin_ref), custom_call_target="tpu_custom_call" | custom-call | flops 8053063680 | bytes 33554432 | tf_op jit(solution)/shard_map/attn_fwd/pallas_call | solution.py:154
  131.8 0.2 all-gather.14.cloned.1.call-start
  132.1 7.9 fusion.98
  140.0 0.5 collective-permute-start.4
  140.5 18.8 %collective-permute-done.1 = f32[4,512,1536]{2,1,0:T(8,128)} collective-permute-done((f32[4,512,1536]{2,1,0:T(8,128)S(1)}, f32[4,512,1536]{2,1,0:T(8,128)}, u32[]{:S(2)}, u32[]{:S(2)}) %collective-permute-start.1) | collective-permute-done | bytes 12582944 | tf_op jit(solution)/shard_map/ppermute | solution.py:203
  159.3 10.8 fusion.60
  170.2 2.6 copy-done
  172.8 4.2 fusion.49
  177.0 0.1 collective-permute-start.2
  177.2 0.3 reduce-scatter.8.cloned.1.call-start
  177.4 11.5 pad_maximum_fusion.2
  189.0 1.5 fusion.108
  190.5 2.7 copy-done.1
  193.2 8.4 pad_maximum_fusion.1
  201.6 11.2 all-gather.10.cloned.1.call-done
  212.8 68.8 %fusion.41 = f32[2,4,512,4480]{3,2,1,0:T(8,128)} fusion(bf16[1536,4480]{1,0:T(8,128)(2,1)} %all-gather.10.cloned.1.call-done, bf16[1,4,512,1536]{3,2,1,0:T(8,128)(2,1)} %bitcast.11, bf16[1,4,512,1536]{3,2,1,0:T(8,128)(2,1)} %copy-done.1), kind=kOutput, calls=%fused_computation.58 | convolution fusion | flops 56377737216 | bytes 99745792 | tf_op jit(solution)/shard_map/tbsd,df->tbsf/dot_general | solution.py:209
  281.6 59.5 %all-gather.12.cloned.1.call-done = bf16[1536,4480]{1,0:T(8,128)(2,1)} async-done(((bf16[384,4480]{1,0:T(8,128)(2,1)}), bf16[1536,4480]{1,0:T(8,128)(2,1)}) %all-gather.12.cloned.1.call-update) | async-done | bytes 13762576 | tf_op jit(solution)/shard_map/all_gather | solution.py:194
  341.1 81.9 %multiply_convert_fusion = (bf16[2,4,512,4480]{3,2,1,0:T(8,128)(2,1)}, f32[2,4,512,4480]{3,2,1,0:T(8,128)}) fusion(f32[2,4,512,4480]{3,2,1,0:T(8,128)} %fusion.41, bf16[1536,4480]{1,0:T(8,128)(2,1)} %all-gather.12.cloned.1.call-done, bf16[1,4,512,1536]{3,2,1,0:T(8,128)(2,1)} %bitcast.11, bf16[1,4,512,1536]{3,2,1,0:T(8,128)(2,1)} %copy-done.1), kind=kOutput, calls=%fused_computation.6 | convolution fusion | flops 56487837696 | bytes 209846272 | tf_op jit(solution)/shard_map/tbsd,df->tbsf/dot_general | solution.py:209
  423.0 67.8 %fusion.17 = f32[4480,1536]{1,0:T(8,128)} fusion(bf16[2,4,512,4480]{3,2,1,0:T(8,128)(2,1)} %get-tuple-element.49, bf16[1,4,512,1536]{3,2,0,1:T(8,128)(2,1)} %bitcast.20, bf16[1,4,512,1536]{3,2,0,1:T(8,128)(2,1)} %bitcast.149), kind=kOutput, calls=%fused_computation.28 | convolution fusion | flops 56377737216 | bytes 76808192 | tf_op jit(solution)/shard_map/tbsf,tbsd->fd/dot_general | solution.py:209
  490.8 97.5 %fusion.2 = (bf16[2,4,512,4480]{3,2,1,0:T(8,128)(2,1)}, bf16[2,4,512,4480]{3,2,1,0:T(8,128)(2,1)}) fusion(f32[2,4,512,4480]{3,2,1,0:T(8,128)} %get-tuple-element.50, f32[2,4,512,4480]{3,2,1,0:T(8,128)} %fusion.41, bf16[4480,1536]{1,0:T(8,128)(2,1)} %all-gather.14.cloned.1.call-done, bf16[2,4,512,1536]{3,2,0,1:T(8,128)(2,1)} %pad_maximum_fusion.2), kind=kOutput, calls=%fused_computation.4 | convolution fusion | flops 56646696960 | bytes 246546432 | tf_op jit(solution)/shard_map/tbsd,fd->tbsf/dot_general | solution.py:209
  588.4 70.8 %fusion.11 = f32[1536,4480]{1,0:T(8,128)} fusion(bf16[2,4,512,4480]{3,2,1,0:T(8,128)(2,1)} %get-tuple-element.33, bf16[1,4,512,1536]{3,2,1,0:T(8,128)(2,1)} %bitcast.11, bf16[1,4,512,1536]{3,2,1,0:T(8,128)(2,1)} %copy-done.1), kind=kOutput, calls=%fused_computation.26 | convolution fusion | flops 56377737216 | bytes 76808192 | tf_op jit(solution)/shard_map/tbsd,tbsf->df/dot_general | solution.py:209
  659.1 70.8 %fusion.14 = f32[1536,4480]{1,0:T(8,128)} fusion(bf16[2,4,512,4480]{3,2,1,0:T(8,128)(2,1)} %get-tuple-element.34, bf16[2,4,512,1536]{3,2,1,0:T(8,128)(2,1)} %pad_maximum_fusion.1), kind=kOutput, calls=%fused_computation.27 | convolution fusion | flops 56371445760 | bytes 76808192 | tf_op jit(solution)/shard_map/tbsd,tbsf->df/dot_general | solution.py:209
  729.9 38.4 %fusion.22 = f32[4,512,1536]{2,1,0:T(8,128)} fusion(bf16[2,4,512,4480]{3,2,1,0:T(8,128)(2,1)} %get-tuple-element.34, bf16[1536,4480]{1,0:T(8,128)(2,1)} %all-gather.12.cloned.1.call-done), kind=kOutput, calls=%fused_computation.35 | convolution fusion | flops 28185722880 | bytes 44695552 | tf_op jit(solution)/shard_map/bsf,df->bsd/dot_general | solution.py:209
  768.3 38.2 %fusion.76 = f32[4,512,1536]{2,1,0:T(8,128)} fusion(f32[4,512,1536]{2,1,0:T(8,128)} %fusion.22, bf16[1536,4480]{1,0:T(8,128)(2,1)} %all-gather.10.cloned.1.call-done, bf16[2,4,512,4480]{3,2,1,0:T(8,128)(2,1)} %get-tuple-element.33), kind=kOutput, calls=%fused_computation.97 | convolution fusion | flops 28188868608 | bytes 57278464 | tf_op jit(solution)/shard_map/bsf,df->bsd/dot_general | solution.py:209
  806.5 38.0 %fusion.26 = f32[4,512,1536]{2,1,0:T(8,128)} fusion(bf16[2,4,512,4480]{3,2,1,0:T(8,128)(2,1)} %get-tuple-element.34, bf16[1536,4480]{1,0:T(8,128)(2,1)} %all-gather.12.cloned.1.call-done), kind=kOutput, calls=%fused_computation.39 | convolution fusion | flops 28185722880 | bytes 44695552 | tf_op jit(solution)/shard_map/bsf,df->bsd/dot_general | solution.py:209
  844.5 41.4 %fusion.51 = (f32[1536]{0:T(1024)}, f32[4,512]{1,0:T(4,128)S(1)}, bf16[4,512,1536]{2,1,0:T(8,128)(2,1)}) fusion(bf16[4,512,1536]{2,1,0:T(8,128)(2,1)} %copy-done, f32[4,512]{1,0:T(4,128)S(1)} %copy-done.6, f32[1536]{0:T(1024)S(1)} %copy-done.8, f32[4,512,1536]{2,1,0:T(8,128)} %collective-permute-done.5, f32[4,512,1536]{2,1,0:T(8,128)} %fusion.26, ...), kind=kOutput, calls=%fused_computation.68 | convolution fusion | flops 28220321792 | bytes 69890048 | tf_op jit(solution)/shard_map/bsf,df->bsd/dot_general | solution.py:209
  886.0 8.6 fusion.54
  894.6 0.5 collective-permute-start.6
  895.1 9.8 collective-permute-done.6
  904.9 2.7 copy-done.17
  907.6 14.7 fusion.89
  922.3 0.0 reduce-scatter.6.cloned.1.call-start
  922.4 15.0 convolution_convert_fusion.1.do_ref
  937.4 92.2 %attn_bwd.1 = bf16[2,4,512,1024]{3,2,1,0:T(8,128)(2,1)} custom-call(s32[1]{0:T(128)} %bitcast.idx_ref, bf16[2,4,512,1024]{3,2,1,0:T(8,128)(2,1)} %get-tuple-element.35.rot_ref, bf16[2,4,512,768]{3,2,1,0:T(8,128)(2,1)} %convolution_convert_fusion.1.do_ref, f32[2,512,128]{2,1,0:T(8,128)} %get-tuple-element.54.cos_ref, f32[2,512,128]{2,1,0:T(8,128)} %get-tuple-element.53.sin_ref), custom_call_target="tpu_custom_call" | custom-call | flops 20132659200 | bytes 25165824 | tf_op jit(solution)/shard_map/attn_bwd/pallas_call | solution.py:173
  1029.7 19.5 %fusion.83 = f32[1536,1024]{1,0:T(8,128)} fusion(bf16[2,4,512,1024]{3,2,1,0:T(8,128)(2,1)} %attn_bwd.1, bf16[1,4,512,1536]{3,2,1,0:T(8,128)(2,1)} %bitcast.2, bf16[1,4,512,1536]{3,2,1,0:T(8,128)(2,1)} %bitcast.153), kind=kOutput, calls=%fused_computation.98 | convolution fusion | flops 12891193344 | bytes 27262976 | tf_op jit(solution)/shard_map/tbsd,tbsc->dc/dot_general | solution.py:209
  1049.2 0.0 reduce-scatter.10.cloned.1.call-start
  1049.3 0.7 reduce-scatter.10.cloned.1.call-update
  1050.0 0.7 reduce-scatter.12.cloned.1.call-update
  1050.7 0.0 reduce-scatter.14.cloned.1.call-start
  1050.7 0.5 reduce-scatter.14.cloned.1.call-update
  1051.3 39.5 %fusion.20 = f32[4,512,1536]{2,1,0:T(8,128)} fusion(bf16[2,4,512,4480]{3,2,1,0:T(8,128)(2,1)} %get-tuple-element.49, bf16[4480,1536]{1,0:T(8,128)(2,1)} %all-gather.14.cloned.1.call-done), kind=kOutput, calls=%fused_computation.32 | convolution fusion | flops 28185722880 | bytes 44695552 | tf_op jit(solution)/shard_map/bsf,fd->bsd/dot_general | solution.py:209
  1090.8 0.5 collective-permute-start.3
  1091.3 12.4 fusion.88
  1103.7 6.7 collective-permute-done.3
  1110.4 38.9 %fusion.61 = bf16[4,512,1536]{2,1,0:T(8,128)(2,1)} fusion(bf16[4,512,1536]{2,1,0:T(8,128)(2,1)} %copy-done, f32[4,512,1536]{2,1,0:T(8,128)} %collective-permute-done.3, bf16[4480,1536]{1,0:T(8,128)(2,1)} %all-gather.14.cloned.1.call-done, bf16[2,4,512,4480]{3,2,1,0:T(8,128)(2,1)} %get-tuple-element.49), kind=kOutput, calls=%fused_computation.78 | convolution fusion | flops 28204597248 | bytes 57278464 | tf_op jit(solution)/shard_map/bsf,fd->bsd/dot_general | solution.py:209
  1149.4 15.5 fusion.52
  1164.9 23.5 %all-reduce = (f32[1536]{0:T(1024)}, f32[1536]{0:T(1024)}) all-reduce(f32[1536]{0:T(1024)S(1)} %get-tuple-element.41, f32[1536]{0:T(1024)S(1)} %copy-done.16), channel_id=1, replica_groups=mesh['fsdp'=4,'model'=2] {'fsdp','model'}, use_global_device_ids=true, to_apply=%region_5.6 | all-reduce | flops 3072 | bytes 24576 | tf_op jit(solution)/shard_map/psum | solution.py:286
  1188.4 11.0 fusion.56
  1199.4 154.7 %reduce-scatter.10.cloned.1.call-done = f32[384,4480]{1,0:T(8,128)} async-done(((f32[1536,4480]{1,0:T(8,128)}), f32[384,4480]{1,0:T(8,128)}) %reduce-scatter.10.cloned.1.call-update) | async-done | bytes 6881296 | tf_op jit(solution)/shard_map/reduce_scatter | solution.py:200
  1354.2 238.9 %reduce-scatter.12.cloned.1.call-done = f32[384,4480]{1,0:T(8,128)} async-done(((f32[1536,4480]{1,0:T(8,128)}), f32[384,4480]{1,0:T(8,128)}) %reduce-scatter.12.cloned.1.call-update) | async-done | bytes 6881296 | tf_op jit(solution)/shard_map/reduce_scatter | solution.py:200
  1593.1 238.8 %reduce-scatter.14.cloned.1.call-done = f32[4480,384]{1,0:T(8,128)} async-done(((f32[4480,1536]{1,0:T(8,128)}), f32[4480,384]{1,0:T(8,128)}) %reduce-scatter.14.cloned.1.call-update) | async-done | bytes 6881296 | tf_op jit(solution)/shard_map/reduce_scatter | solution.py:200
  (75 shorter events, 0.5 us)
Async XLA Ops:
  7.2 14.1 copy-start.3
  7.2 43.7 %all-gather.6.cloned.1.call-start = ((), (), s32[]{:S(2)}) async-start(), calls=%async_computation.5 | async-start | bytes 3932160 | tf_op jit(solution)/shard_map/all_gather | solution.py:194
  7.9 124.2 %all-gather.8.cloned.1.call-start = ((), (), s32[]{:S(2)}) async-start(), calls=%async_computation.6 | async-start | bytes 2949120 | tf_op jit(solution)/shard_map/all_gather | solution.py:197
  8.7 12.9 copy-start.4
  8.7 204.1 %all-gather.10.cloned.1.call-start = ((), (), s32[]{:S(2)}) async-start(), calls=%async_computation.7 | async-start | bytes 17203200 | tf_op jit(solution)/shard_map/all_gather | solution.py:194
  12.8 8.5 copy-start.11
  12.9 8.4 copy-start.9
  19.9 321.2 %all-gather.12.cloned.1.call-start = ((), (), s32[]{:S(2)}) async-start(), calls=%async_computation.8 | async-start | bytes 17203200 | tf_op jit(solution)/shard_map/all_gather | solution.py:194
  20.5 30.4 %collective-permute-start = (bf16[4,512,1536]{2,1,0:T(8,128)(2,1)}, bf16[4,512,1536]{2,1,0:T(8,128)(2,1)}, u32[]{:S(2)}, u32[]{:S(2)}) collective-permute-start(bf16[4,512,1536]{2,1,0:T(8,128)(2,1)} %fusion.50), channel_id=1, source_target_pairs={{0,1},{1,0},{2,3},{3,2},{4,5},{5,4},{6,7},{7,6}} | collective-permute-start | bytes 18874376 | tf_op jit(solution)/shard_map/ppermute | solution.py:203
  131.8 359.0 %all-gather.14.cloned.1.call-start = ((), (), s32[]{:S(2)}) async-start(), calls=%async_computation.9 | async-start | bytes 17203200 | tf_op jit(solution)/shard_map/all_gather | solution.py:197
  132.1 27.2 %copy-start.19 = (bf16[768,1536]{1,0:T(8,128)(2,1)S(1)}, bf16[768,1536]{1,0:T(8,128)(2,1)}, u32[]{:S(2)}) copy-start(bf16[768,1536]{1,0:T(8,128)(2,1)} %all-gather.8.cloned.1.call-done) | copy-start | bytes 7077892
  140.0 32.8 %copy-start.7 = (f32[1536]{0:T(1024)S(1)}, f32[1536]{0:T(1024)}, u32[]{:S(2)}) copy-start(f32[1536]{0:T(1024)} %param.14) | copy-start | bytes 18436
  140.0 19.3 %collective-permute-start.1 = (f32[4,512,1536]{2,1,0:T(8,128)S(1)}, f32[4,512,1536]{2,1,0:T(8,128)}, u32[]{:S(2)}, u32[]{:S(2)}) collective-permute-start(f32[4,512,1536]{2,1,0:T(8,128)S(1)} %fusion.98), channel_id=1, source_target_pairs={{0,1},{1,0},{2,3},{3,2},{4,5},{5,4},{6,7},{7,6}} | collective-permute-start | bytes 37748744 | tf_op jit(solution)/shard_map/ppermute | solution.py:203
  140.0 37.4 %collective-permute-start.4 = (bf16[4,512,1536]{2,1,0:T(8,128)(2,1)}, bf16[4,512,1536]{2,1,0:T(8,128)(2,1)}, u32[]{:S(2)}, u32[]{:S(2)}) collective-permute-start(bf16[4,512,1536]{2,1,0:T(8,128)(2,1)} %param.12), channel_id=1, source_target_pairs={{0,1},{1,0},{2,3},{3,2},{4,5},{5,4},{6,7},{7,6}} | collective-permute-start | bytes 18874376 | tf_op jit(solution)/shard_map/ppermute | solution.py:203
  170.2 2.6 copy-start
  170.2 6.8 copy-start.14
  170.2 18.8 %copy-start.5 = (f32[4,512]{1,0:T(4,128)}, f32[4,512]{1,0:T(4,128)S(1)}, u32[]{:S(2)}) copy-start(f32[4,512]{1,0:T(4,128)S(1)} %fusion.107) | copy-start | bytes 24580
  177.0 13.5 collective-permute-start.2
  177.1 11.8 slice-start.2
  177.2 1022.3 %reduce-scatter.8.cloned.1.call-start = ((), (), s32[]{:S(2)}) async-start(), calls=%async_computation.11 | async-start | bytes 5898240 | tf_op jit(solution)/shard_map/reduce_scatter | solution.py:200
  177.4 11.5 slice-start.3
  190.5 2.7 copy-start.1
  806.5 38.0 %copy-start.6 = (f32[4,512]{1,0:T(4,128)S(1)}, f32[4,512]{1,0:T(4,128)}, u32[]{:S(2)}) copy-start(f32[4,512]{1,0:T(4,128)} %copy-done.5) | copy-start | bytes 24580
  806.5 38.0 %copy-start.8 = (f32[1536]{0:T(1024)S(1)}, f32[1536]{0:T(1024)}, u32[]{:S(2)}) copy-start(f32[1536]{0:T(1024)} %param.14) | copy-start | bytes 18436
  806.5 38.0 %collective-permute-start.5 = (f32[4,512,1536]{2,1,0:T(8,128)}, f32[4,512,1536]{2,1,0:T(8,128)}, u32[]{:S(2)}, u32[]{:S(2)}) collective-permute-start(f32[4,512,1536]{2,1,0:T(8,128)} %fusion.76), channel_id=1, source_target_pairs={{0,1},{1,0},{2,3},{3,2},{4,5},{5,4},{6,7},{7,6}} | collective-permute-start | bytes 37748744 | tf_op jit(solution)/shard_map/ppermute | solution.py:203
  844.5 41.5 %copy-start.15 = (f32[4,512]{1,0:T(4,128)S(1)}, f32[4,512]{1,0:T(4,128)}, u32[]{:S(2)}) copy-start(f32[4,512]{1,0:T(4,128)} %copy-done.14) | copy-start | bytes 24580
  894.6 10.3 copy-start.2
  894.6 10.3 collective-permute-start.6
  904.9 2.7 copy-start.17
  907.6 14.8 copy-start.20
  922.3 277.1 %reduce-scatter.6.cloned.1.call-start = ((), (), s32[]{:S(2)}) async-start(), calls=%async_computation.10 | async-start | bytes 7864320 | tf_op jit(solution)/shard_map/reduce_scatter | solution.py:200
  1049.2 305.0 %reduce-scatter.10.cloned.1.call-start = ((), (), s32[]{:S(2)}) async-start(), calls=%async_computation.12 | async-start | bytes 34406400 | tf_op jit(solution)/shard_map/reduce_scatter | solution.py:200
  1050.0 543.1 %reduce-scatter.12.cloned.1.call-start = ((), (), s32[]{:S(2)}) async-start(), calls=%async_computation.13 | async-start | bytes 34406400 | tf_op jit(solution)/shard_map/reduce_scatter | solution.py:200
  1050.7 781.2 %reduce-scatter.14.cloned.1.call-start = ((), (), s32[]{:S(2)}) async-start(), calls=%async_computation.14 | async-start | bytes 34406400 | tf_op jit(solution)/shard_map/reduce_scatter | solution.py:200
  1051.3 40.0 %copy-start.18 = (bf16[1536,1024]{1,0:T(8,128)(2,1)S(1)}, bf16[1536,1024]{1,0:T(8,128)(2,1)}, u32[]{:S(2)}) copy-start(bf16[1536,1024]{1,0:T(8,128)(2,1)} %all-gather.6.cloned.1.call-done) | copy-start | bytes 9437188
  1090.8 19.6 %collective-permute-start.3 = (f32[4,512,1536]{2,1,0:T(8,128)}, f32[4,512,1536]{2,1,0:T(8,128)}, u32[]{:S(2)}, u32[]{:S(2)}) collective-permute-start(f32[4,512,1536]{2,1,0:T(8,128)} %fusion.20), channel_id=1, source_target_pairs={{0,1},{1,0},{2,3},{3,2},{4,5},{5,4},{6,7},{7,6}} | collective-permute-start | bytes 37748744 | tf_op jit(solution)/shard_map/ppermute | solution.py:203
  1091.3 58.0 %slice-start = ((s8[6291456]{0:T(1024)(128)(4,1)}), s8[4194304]{0:T(1024)(128)(4,1)S(1)}, s32[]{:S(2)}) async-start(s8[6291456]{0:T(1024)(128)(4,1)} %bitcast.144), calls=%async_computation.15 | async-start | bytes 8388608
  1103.7 45.6 %slice-start.1 = ((s8[6291456]{0:T(1024)(128)(4,1)}), s8[2097152]{0:T(1024)(128)(4,1)S(1)}, s32[]{:S(2)}) async-start(s8[6291456]{0:T(1024)(128)(4,1)} %bitcast.144), calls=%async_computation.16 | async-start | bytes 4194304
  1103.7 45.6 %copy-start.10 = (f32[4,512]{1,0:T(4,128)S(1)}, f32[4,512]{1,0:T(4,128)}, u32[]{:S(2)}) copy-start(f32[4,512]{1,0:T(4,128)} %copy-done.9) | copy-start | bytes 24580
  1103.7 45.7 %copy-start.13 = (f32[1536]{0:T(1024)S(1)}, f32[1536]{0:T(1024)}, u32[]{:S(2)}) copy-start(f32[1536]{0:T(1024)} %param.13) | copy-start | bytes 18436
  1103.7 45.6 %collective-permute-start.7 = (f32[4,512,1536]{2,1,0:T(8,128)}, f32[4,512,1536]{2,1,0:T(8,128)}, u32[]{:S(2)}, u32[]{:S(2)}) collective-permute-start(f32[4,512,1536]{2,1,0:T(8,128)} %fusion.88), channel_id=1, source_target_pairs={{0,1},{1,0},{2,3},{3,2},{4,5},{5,4},{6,7},{7,6}} | collective-permute-start | bytes 37748744 | tf_op jit(solution)/shard_map/ppermute | solution.py:203
  1149.3 15.6 copy-start.16
  1149.3 39.1 %copy-start.12 = (f32[4,512]{1,0:T(4,128)S(1)}, f32[4,512]{1,0:T(4,128)}, u32[]{:S(2)}) copy-start(f32[4,512]{1,0:T(4,128)} %copy-done.11) | copy-start | bytes 24580
Sparse Core Ops, SparseCore 0:
  9.8 41.0 all-gather.5
  52.6 31.6 all-gather.7
  86.1 126.6 all-gather.9
  214.4 126.6 all-gather.11
  342.7 126.5 all-gather.13
  922.5 51.2 reduce-scatter.7
  1049.3 64.4 reduce-scatter.5
  1117.4 236.6 reduce-scatter.9
  1357.8 235.2 reduce-scatter.11
  1596.5 235.2 reduce-scatter.13

commit v2 on v1

--- a/solution.py
+++ b/solution.py
@@ -139,6 +139,11 @@
         dqkv_ref[st, 0, :, vcol:vcol + dim] = dv_scr[rows, :].astype(jnp.bfloat16)
 
 
+def blank(shape, dtype):
+    return pl.pallas_call(lambda out_ref: None, out_shape=jax.ShapeDtypeStruct(shape, dtype),
+                          out_specs=pl.BlockSpec(memory_space=pl.ANY))()
+
+
 def seq_block(rows, cols):
     return pl.BlockSpec((2, 1, rows, cols), lambda b, idx: (0, b, 0, 0))
 
@@ -190,6 +195,26 @@
     cols_spec = P('model', 'fsdp')
     swap = [(0, 1), (1, 0)]
 
+    along_x = [(0, 1), (1, 0), (2, 3), (3, 2)]
+    along_y = [(0, 2), (2, 0), (1, 3), (3, 1)]
+
+    def hop(tensor, pairs):
+        return lax.ppermute(tensor, 'fsdp', pairs)
+
+    def ring_gather(shard):
+        me = lax.axis_index('fsdp')
+        rows = shard.shape[0]
+        half = rows // 2
+        upper, lower = shard[:half], shard[half:]
+        y_upper, x_lower = hop(upper, along_y), hop(lower, along_x)
+        x_upper, y_lower = hop(upper, along_x), hop(lower, along_y)
+        d_upper, d_lower = hop(y_upper, along_x), hop(x_lower, along_y)
+        full = jnp.zeros((4 * rows, shard.shape[1]), shard.dtype)
+        for offset, parts in ((0, (upper, lower)), (1, (x_upper, x_lower)), (2, (y_upper, y_lower)), (3, (d_upper, d_lower))):
+            start = (me ^ offset) * rows
+            full = lax.dynamic_update_slice(full, jnp.concatenate(parts), (start, 0))
+        return full
+
     def gather_rows(w_shard):
         return lax.all_gather(w_shard, 'fsdp', axis=0, tiled=True)
 
@@ -203,7 +228,10 @@
         return lax.ppermute(tensor, 'model', swap)
 
     def both(own):
-        return jnp.stack([own, partner(own)])
+        other = partner(own)
+        pair = blank((2,) + own.shape, own.dtype)
+        pair = lax.dynamic_update_slice(pair, own[None], (0, 0, 0, 0))
+        return lax.dynamic_update_slice(pair, other[None], (1, 0, 0, 0))
 
     def dot(spec, left, right):
         return jnp.einsum(spec, left, right, preferred_element_type=jnp.float32)
@@ -222,24 +250,23 @@
         cos_t = table(rope_cos, rope_cos)
         sin_t = table(-rope_sin, rope_sin)
 
-        w_qkv = gather_rows(wqkv_sh)
-        w_out = gather_cols(wout_sh)
+        w_qkv = ring_gather(wqkv_sh)
+        w_gate = gather_rows(wgate_sh)
 
         x_f32 = x_loc.astype(jnp.float32)
         h_attn_f, norm_back_attn = jax.vjp(rms_scale, x_f32, gain_attn)
         h_own = h_attn_f.astype(jnp.bfloat16)
-        wgate_sh, h_own = lax.optimization_barrier((wgate_sh, h_own))
-        w_gate = gather_rows(wgate_sh)
-        h_attn = both(h_own)
-        dy = both(dy_loc)
+        h_attn, dy = lax.optimization_barrier((both(h_own), both(dy_loc)))
         qkv = dot('tbsd,dc->tbsc', h_attn, w_qkv)
         wup_sh, qkv = lax.optimization_barrier((wup_sh, qkv))
         w_up = gather_rows(wup_sh)
+        w_out_t = ring_gather(wout_sh.T)
         rot, attn = attn_fwd(idx, qkv, cos_t, sin_t, heads)
         wdown_sh, attn = lax.optimization_barrier((wdown_sh, attn))
         w_down = gather_cols(wdown_sh)
-        out_other = partner(dot('bsh,hd->bsd', attn[1], w_out))
-        attn_red = dot('bsh,hd->bsd', attn[0], w_out) + out_other
+        heads_other, w_out_other = partner(attn[1]), partner(w_out_t)
+        own_heads = lax.optimization_barrier(dot('bsh,dh->bsd', attn[0], w_out_t))
+        attn_red = own_heads + dot('bsh,dh->bsd', heads_other, w_out_other)
         mid_f32 = (x_f32 + attn_red.astype(jnp.bfloat16).astype(jnp.float32)).astype(jnp.bfloat16).astype(jnp.float32)
         h_mlp_f, norm_back_mlp = jax.vjp(rms_scale, mid_f32, gain_mlp)
         h_mlp = both(h_mlp_f.astype(jnp.bfloat16))
@@ -255,10 +282,12 @@
         d_act = dot('tbsd,fd->tbsf', dy, w_down).astype(jnp.bfloat16).astype(jnp.float32)
         d_gate = (d_act * up_proj * sig_gate * (1.0 + gate * (1.0 - sig_gate))).astype(jnp.bfloat16)
         d_up = (d_act * silu_gate).astype(jnp.bfloat16)
-        full_gate, h_mlp = lax.optimization_barrier((dot('tbsd,tbsf->df', h_mlp, d_gate), h_mlp))
-        dw_gate = scatter(full_gate, 0)
-        full_up, d_gate, d_up = lax.optimization_barrier((dot('tbsd,tbsf->df', h_mlp, d_up), d_gate, d_up))
-        dw_up = scatter(full_up, 0)
+        pair = blank((2,) + w_gate.shape, jnp.float32)
+        pair = lax.dynamic_update_slice(pair, dot('tbsd,tbsf->df', h_mlp, d_gate)[None], (0, 0, 0))
+        pair, h_mlp = lax.optimization_barrier((pair, h_mlp))
+        pair = lax.dynamic_update_slice(pair, dot('tbsd,tbsf->df', h_mlp, d_up)[None], (1, 0, 0))
+        pair, d_gate, d_up = lax.optimization_barrier((pair, d_gate, d_up))
+        dw_gate, dw_up = scatter(pair, 1)
 
         def dh_of(part):
             return (dot('bsf,df->bsd', d_gate[part], w_gate)
@@ -270,10 +299,12 @@
         d_mid = (dy_loc.astype(jnp.float32) + d_mid_norm).astype(jnp.bfloat16)
         d_mid_full = both(d_mid)
 
-        d_attn = dot('tbsd,hd->tbsh', d_mid_full, w_out).astype(jnp.bfloat16)
+        d_attn = dot('tbsd,dh->tbsh', d_mid_full, w_out_t).astype(jnp.bfloat16)
+        full_out, d_attn = lax.optimization_barrier((dot('tbsd,tbsh->dh', d_mid_full, attn), d_attn))
         d_qkv = attn_bwd(idx, rot, d_attn, cos_t, sin_t, heads)
-        dw_out = scatter(dot('tbsh,tbsd->hd', attn, d_mid_full), 1)
-        dw_qkv = scatter(dot('tbsd,tbsc->dc', h_attn, d_qkv), 0)
+        full_qkv = dot('tbsd,tbsc->dc', h_attn, d_qkv)
+        both_grads = scatter(jnp.concatenate([full_qkv, full_out], axis=1), 0)
+        dw_qkv, dw_out = both_grads[:, :full_qkv.shape[1]], both_grads[:, full_qkv.shape[1]:].T
         dha_other = partner(dot('bsc,dc->bsd', d_qkv[1], w_qkv))
         dh_attn = dot('bsc,dc->bsd', d_qkv[0], w_qkv) + dha_other
         d_x_norm, d_gain_attn = norm_back_attn(dh_attn.astype(jnp.bfloat16).astype(jnp.float32))

time: 1840 us -> 1880 us (1.022)
  local copies, waits for them, and re-layouts: 8.44 us -> 67.4 us
  waiting for transfers between devices: 770 us -> 728 us
    all_gather x3 -> x2, waiting for transfers between devices: 98.7 us -> 0.01 us  [gather_rows(): return lax.all_gather(w_shard, 'fsdp', axis=0, tiled=True)]
    ppermute x0 -> x12, waiting for transfers between devices: none -> 62.1 us  [hop(): return lax.ppermute(tensor, 'fsdp', pairs)]
    dynamic_update_slice x0 -> x9, other arithmetic: none -> 33 us  [the longest x3 30.2 us: both(): pair = lax.dynamic_update_slice(pair, own[None], (0, 0, 0, 0))]
    dynamic_update_slice x0 -> x7, local copies, waits for them, and re-layouts: none -> 31.4 us  [the longest x4 24.6 us: both(): return lax.dynamic_update_slice(pair, other[None], (1, 0, 0, 0))]
    another operation x3 -> x0, other arithmetic: 21.4 us -> none  [both(): return jnp.stack([own, partner(own)])]
    convert_element_type x3 -> x0, other arithmetic: 19.7 us -> none  [the longest x1 8.56 us: device_fn(): d_mid = (dy_loc.astype(jnp.float32) + d_mid_norm).astype(jnp.bfloat16)]
    reduce_scatter x5 -> x3, waiting for transfers between devices: 632 us -> 636 us  [scatter(): return lax.psum_scatter(tensor, 'fsdp', scatter_dimension=dim, tiled=True)]
  transfers between devices with their start and end apart: 18 -> 27, of which waited for: 9 -> 13; matrix products, arithmetic and copies ran while one was open for 26% -> 26% of each run, Pallas kernels for 8% -> 3%
where the time goes in v2:
time: 1880 us; the launch traced here: 1870 us
  matrix products  805 us (43%)
  waiting for transfers between devices  728 us (39%)
  Pallas kernels  153 us (8%)
  local copies, waits for them, and re-layouts  67.4 us (4%)
  other arithmetic  59.4 us (3%)
  blocking collectives  23.7 us (1%)
  starting transfers between devices  21.2 us (1%)
    dot_general x20, matrix products, dot(): return jnp.einsum(spec, left, right, preferred_element_type=jnp.float32)  805 us
    reduce_scatter x3, waiting for transfers between devices, scatter(): return lax.psum_scatter(tensor, 'fsdp', scatter_dimension=dim, tiled=True)  636 us
    pallas_call x1, Pallas kernels, attn_bwd(): pl.pallas_call(functools.partial(attn_bwd_kernel, heads, 2 * rows, dim),...  92.1 us
    ppermute x12, waiting for transfers between devices, hop(): return lax.ppermute(tensor, 'fsdp', pairs)  62.1 us
    pallas_call x1, Pallas kernels, attn_fwd(): pl.pallas_call(functools.partial(attn_fwd_kernel, heads, 2 * rows, dim),...  60.4 us
  transfers between devices with their start and end apart: 27, of which 13 were waited for; matrix products, arithmetic and copies ran while one was open for 26% of the time, Pallas kernels for 3%

profile of v2, /device:TPU:0, one launch (start us, length us, event | category | flops | bytes accessed | tf_op | source)
XLA Modules:
  0.0 1871.8 jit_solution(7314825914250825378)
XLA Ops:
  8.0 4.2 fusion.55
  12.2 10.7 bitcast_dynamic-update-slice_fusion.9
  23.8 3.0 collective-permute-start.3
  26.8 2.0 collective-permute-start.4
  28.8 16.3 collective-permute-done.3
  45.2 2.0 collective-permute-start.5
  47.2 5.9 bitcast_dynamic-update-slice_fusion.7
  53.1 1.5 collective-permute-start.6
  54.5 7.5 collective-permute-done.2
  62.0 2.0 collective-permute-start.7
  65.5 13.1 collective-permute-done.6
  78.7 3.4 collective-permute-done.7
  82.1 7.4 bitcast_dynamic-update-slice_fusion.8
  89.5 7.8 bitcast_dynamic-update-slice_fusion.6
  97.3 2.2 copy-done.2
  99.5 15.7 fusion.92.qkv_ref
  116.1 1.9 collective-permute-start.9
  118.0 1.5 collective-permute-start.10
  119.8 1.1 pad_maximum_fusion.1
  122.1 60.4 %attn_fwd.1 = (bf16[2,4,512,1024]{3,2,1,0:T(8,128)(2,1)}, bf16[2,4,512,768]{3,2,1,0:T(8,128)(2,1)}) custom-call(s32[1]{0:T(128)} %bitcast.idx_ref, f32[2,4,512,1024]{3,2,1,0:T(8,128)} %fusion.92.qkv_ref, f32[2,512,128]{2,1,0:T(8,128)} %get-tuple-element.79.cos_ref, f32[2,512,128]{2,1,0:T(8,128)} %get-tuple-element.78.sin_ref), custom_call_target="tpu_custom_call" | custom-call | flops 8053063680 | bytes 33554432 | tf_op jit(solution)/shard_map/attn_fwd/pallas_call | solution.py:159
  182.6 4.4 slice_bitcast_fusion.12
  187.6 1.8 collective-permute-start.12
  189.4 1.6 collective-permute-start.13
  191.0 1.6 broadcast_in_dim.51
  193.4 9.7 collective-permute-done.8
  204.9 10.8 collective-permute-done.12
  216.9 10.2 fusion.96
  227.1 11.8 fusion.58
  240.2 8.9 bitcast_dynamic-update-slice_fusion.5
  249.8 9.9 collective-permute-done.16
  259.7 5.9 bitcast_dynamic-update-slice_fusion.4
  265.6 68.5 %fusion.39 = f32[2,4,512,4480]{3,2,1,0:T(8,128)} fusion(bf16[2,4,512,1536]{3,2,1,0:T(8,128)(2,1)} %bitcast_dynamic-update-slice_fusion.4, bf16[1536,4480]{1,0:T(8,128)(2,1)} %all-gather.4.cloned.1.call-done), kind=kOutput, calls=%fused_computation.58 | convolution fusion | flops 56371445760 | bytes 99745792 | tf_op jit(solution)/shard_map/tbsd,df->tbsf/dot_general | solution.py:237
  334.1 84.2 %multiply_convert_fusion = (bf16[2,4,512,4480]{3,2,1,0:T(8,128)(2,1)}, f32[2,4,512,4480]{3,2,1,0:T(8,128)}) fusion(f32[2,4,512,4480]{3,2,1,0:T(8,128)} %fusion.39, bf16[2,4,512,1536]{3,2,1,0:T(8,128)(2,1)} %bitcast_dynamic-update-slice_fusion.4, bf16[1536,4480]{1,0:T(8,128)(2,1)} %all-gather.6.cloned.1.call-done), kind=kOutput, calls=%fused_computation.6 | convolution fusion | flops 56481546240 | bytes 209846272 | tf_op jit(solution)/shard_map/tbsd,df->tbsf/dot_general | solution.py:237
  418.2 67.7 %fusion.15 = f32[4480,1536]{1,0:T(8,128)} fusion(bf16[2,4,512,4480]{3,2,1,0:T(8,128)(2,1)} %get-tuple-element.74, bf16[2,4,512,1536]{3,2,1,0:T(8,128)(2,1)} %bitcast_dynamic-update-slice_fusion.6), kind=kOutput, calls=%fused_computation.28 | convolution fusion | flops 56371445760 | bytes 76808192 | tf_op jit(solution)/shard_map/tbsf,tbsd->fd/dot_general | solution.py:237
  485.9 97.2 %fusion.3 = (bf16[2,4,512,4480]{3,2,1,0:T(8,128)(2,1)}, bf16[2,4,512,4480]{3,2,1,0:T(8,128)(2,1)}) fusion(f32[2,4,512,4480]{3,2,1,0:T(8,128)} %fusion.39, f32[2,4,512,4480]{3,2,1,0:T(8,128)} %get-tuple-element.75, bf16[2,4,512,1536]{3,2,1,0:T(8,128)(2,1)} %bitcast_dynamic-update-slice_fusion.6, bf16[4480,1536]{1,0:T(8,128)(2,1)} %all-gather.8.cloned.1.call-done), kind=kOutput, calls=%fused_computation.5 | convolution fusion | flops 56646696960 | bytes 246546432 | tf_op jit(solution)/shard_map/tbsd,fd->tbsf/dot_general | solution.py:237
  583.2 70.6 %bitcast_dynamic-update-slice_fusion.1 = f32[2,1536,4480]{2,1,0:T(8,128)} fusion(f32[2,1536,4480]{2,1,0:T(8,128)} %shard_map.181, bf16[2,4,512,4480]{3,2,1,0:T(8,128)(2,1)} %get-tuple-element.36, bf16[2,4,512,1536]{3,2,1,0:T(8,128)(2,1)} %bitcast_dynamic-update-slice_fusion.4), kind=kOutput, calls=%fused_computation.16 | convolution fusion | flops 56371445760 | bytes 76808192 | tf_op jit(solution)/shard_map/tbsd,tbsf->df/dot_general | solution.py:237
  653.8 70.8 %bitcast_dynamic-update-slice_fusion = f32[2,1536,4480]{2,1,0:T(8,128)} fusion(f32[2,1536,4480]{2,1,0:T(8,128)} %bitcast_dynamic-update-slice_fusion.1, bf16[2,4,512,4480]{3,2,1,0:T(8,128)(2,1)} %get-tuple-element.37, bf16[2,4,512,1536]{3,2,1,0:T(8,128)(2,1)} %bitcast_dynamic-update-slice_fusion.4), kind=kOutput, calls=%fused_computation.15 | convolution fusion | flops 56371445760 | bytes 76808192 | tf_op jit(solution)/shard_map/tbsd,tbsf->df/dot_general | solution.py:237
  724.5 38.4 %fusion.20 = f32[4,512,1536]{2,1,0:T(8,128)} fusion(bf16[2,4,512,4480]{3,2,1,0:T(8,128)(2,1)} %get-tuple-element.37, bf16[1536,4480]{1,0:T(8,128)(2,1)} %all-gather.6.cloned.1.call-done), kind=kOutput, calls=%fused_computation.35 | convolution fusion | flops 28185722880 | bytes 44695552 | tf_op jit(solution)/shard_map/bsf,df->bsd/dot_general | solution.py:237
  762.9 38.2 %fusion.74 = f32[4,512,1536]{2,1,0:T(8,128)} fusion(f32[4,512,1536]{2,1,0:T(8,128)} %fusion.20, bf16[1536,4480]{1,0:T(8,128)(2,1)} %all-gather.4.cloned.1.call-done, bf16[2,4,512,4480]{3,2,1,0:T(8,128)(2,1)} %get-tuple-element.36), kind=kOutput, calls=%fused_computation.104 | convolution fusion | flops 28188868608 | bytes 57278464 | tf_op jit(solution)/shard_map/bsf,df->bsd/dot_general | solution.py:237
  801.5 38.0 %fusion.24 = f32[4,512,1536]{2,1,0:T(8,128)} fusion(bf16[2,4,512,4480]{3,2,1,0:T(8,128)(2,1)} %get-tuple-element.37, bf16[1536,4480]{1,0:T(8,128)(2,1)} %all-gather.6.cloned.1.call-done), kind=kOutput, calls=%fused_computation.39 | convolution fusion | flops 28185722880 | bytes 44695552 | tf_op jit(solution)/shard_map/bsf,df->bsd/dot_general | solution.py:237
  839.4 41.4 %fusion.49 = (f32[1536]{0:T(1024)}, f32[4,512]{1,0:T(4,128)S(1)}, bf16[4,512,1536]{2,1,0:T(8,128)(2,1)}) fusion(bf16[4,512,1536]{2,1,0:T(8,128)(2,1)} %get-tuple-element.73, f32[4,512]{1,0:T(4,128)S(1)} %copy-done.13, f32[1536]{0:T(1024)S(1)} %copy-done.19, f32[4,512,1536]{2,1,0:T(8,128)} %collective-permute-done.18, f32[4,512,1536]{2,1,0:T(8,128)} %fusion.24, ...), kind=kOutput, calls=%fused_computation.68 | convolution fusion | flops 28220321792 | bytes 69890048 | tf_op jit(solution)/shard_map/bsf,df->bsd/dot_general | solution.py:237
  880.8 10.6 bitcast_dynamic-update-slice_fusion.3
  891.4 2.7 copy-done
  894.2 10.0 collective-permute-done.19
  904.3 3.5 bitcast_dynamic-update-slice_fusion.2
  907.8 15.4 convolution_convert_fusion.1.do_ref
  923.3 12.3 fusion.87
  935.6 92.1 %attn_bwd.1 = bf16[2,4,512,1024]{3,2,1,0:T(8,128)(2,1)} custom-call(s32[1]{0:T(128)} %bitcast.idx_ref, bf16[2,4,512,1024]{3,2,1,0:T(8,128)(2,1)} %get-tuple-element.38.rot_ref, bf16[2,4,512,768]{3,2,1,0:T(8,128)(2,1)} %convolution_convert_fusion.1.do_ref, f32[2,512,128]{2,1,0:T(8,128)} %get-tuple-element.79.cos_ref, f32[2,512,128]{2,1,0:T(8,128)} %get-tuple-element.78.sin_ref), custom_call_target="tpu_custom_call" | custom-call | flops 20132659200 | bytes 25165824 | tf_op jit(solution)/shard_map/attn_bwd/pallas_call | solution.py:178
  1027.7 19.6 %fusion.81 = f32[1536,1024]{0,1:T(8,128)} fusion(bf16[2,4,512,1024]{3,2,1,0:T(8,128)(2,1)} %attn_bwd.1, bf16[2,4,512,1536]{3,2,1,0:T(8,128)(2,1)} %bitcast_dynamic-update-slice_fusion.8), kind=kOutput, calls=%fused_computation.105 | convolution fusion | flops 12884901888 | bytes 27262976 | tf_op jit(solution)/shard_map/tbsd,tbsc->dc/dot_general | solution.py:237
  1047.3 6.0 copy.33
  1053.4 9.4 pad_maximum_fusion
  1064.0 39.5 %fusion.18 = f32[4,512,1536]{2,1,0:T(8,128)} fusion(bf16[2,4,512,4480]{3,2,1,0:T(8,128)(2,1)} %get-tuple-element.74, bf16[4480,1536]{1,0:T(8,128)(2,1)} %all-gather.8.cloned.1.call-done), kind=kOutput, calls=%fused_computation.32 | convolution fusion | flops 28185722880 | bytes 44695552 | tf_op jit(solution)/shard_map/bsf,fd->bsd/dot_general | solution.py:237
  1103.5 11.8 fusion.86
  1115.6 7.3 collective-permute-done.17
  1122.9 39.0 %fusion.59 = bf16[4,512,1536]{2,1,0:T(8,128)(2,1)} fusion(bf16[4,512,1536]{2,1,0:T(8,128)(2,1)} %get-tuple-element.73, f32[4,512,1536]{2,1,0:T(8,128)} %collective-permute-done.17, bf16[4480,1536]{1,0:T(8,128)(2,1)} %all-gather.8.cloned.1.call-done, bf16[2,4,512,4480]{3,2,1,0:T(8,128)(2,1)} %get-tuple-element.74), kind=kOutput, calls=%fused_computation.78 | convolution fusion | flops 28204597248 | bytes 57278464 | tf_op jit(solution)/shard_map/bsf,fd->bsd/dot_general | solution.py:237
  1161.9 15.2 fusion.50
  1177.1 23.7 %all-reduce = (f32[1536]{0:T(1024)}, f32[1536]{0:T(1024)}) all-reduce(f32[1536]{0:T(1024)S(1)} %get-tuple-element.54, f32[1536]{0:T(1024)S(1)} %copy-done.20), channel_id=1, replica_groups=mesh['fsdp'=4,'model'=2] {'fsdp','model'}, use_global_device_ids=true, to_apply=%region_5.6 | all-reduce | flops 3072 | bytes 24576 | tf_op jit(solution)/shard_map/psum | solution.py:317
  1200.9 10.7 fusion.54
  1211.6 1.5 slice.72
  1213.1 1.6 copy.34
  1214.7 2.4 slice_bitcast_fusion.13
  1217.1 409.0 %reduce-scatter.6.cloned.1.call-done = f32[2,384,4480]{2,1,0:T(8,128)} async-done(((f32[2,1536,4480]{2,1,0:T(8,128)}), f32[2,384,4480]{2,1,0:T(8,128)}) %reduce-scatter.6.cloned.1.call-update) | async-done | bytes 13762576 | tf_op jit(solution)/shard_map/reduce_scatter | solution.py:225
  1626.1 11.3 slice_bitcast_fusion.4
  1637.4 227.5 %reduce-scatter.8.cloned.1.call-done = f32[4480,384]{1,0:T(8,128)} async-done(((f32[4480,1536]{1,0:T(8,128)}), f32[4480,384]{1,0:T(8,128)}) %reduce-scatter.8.cloned.1.call-update) | async-done | bytes 6881296 | tf_op jit(solution)/shard_map/reduce_scatter | solution.py:225
  (121 shorter events, 14.1 us)
Async XLA Ops:
  7.2 5.0 copy-start.14
  7.2 258.4 %all-gather.4.cloned.1.call-start = ((), (), s32[]{:S(2)}) async-start(), calls=%async_computation.3 | async-start | bytes 17203200 | tf_op jit(solution)/shard_map/all_gather | solution.py:219
  7.9 326.2 %all-gather.6.cloned.1.call-start = ((), (), s32[]{:S(2)}) async-start(), calls=%async_computation.4 | async-start | bytes 17203200 | tf_op jit(solution)/shard_map/all_gather | solution.py:219
  8.0 15.8 copy-start.3
  12.1 14.7 copy-start.10
  12.2 14.6 copy-start.8
  22.9 59.2 %collective-permute-start = (bf16[4,512,1536]{2,1,0:T(8,128)(2,1)}, bf16[4,512,1536]{2,1,0:T(8,128)(2,1)}, u32[]{:S(2)}, u32[]{:S(2)}) collective-permute-start(bf16[4,512,1536]{2,1,0:T(8,128)(2,1)} %get-tuple-element.63), channel_id=1, source_target_pairs={{0,1},{1,0},{2,3},{3,2},{4,5},{5,4},{6,7},{7,6}} | collective-permute-start | bytes 18874376 | tf_op jit(solution)/shard_map/ppermute | solution.py:228
  23.7 65.8 %collective-permute-start.1 = (bf16[4,512,1536]{2,1,0:T(8,128)(2,1)}, bf16[4,512,1536]{2,1,0:T(8,128)(2,1)}, u32[]{:S(2)}, u32[]{:S(2)}) collective-permute-start(bf16[4,512,1536]{2,1,0:T(8,128)(2,1)} %param.12), channel_id=1, source_target_pairs={{0,1},{1,0},{2,3},{3,2},{4,5},{5,4},{6,7},{7,6}} | collective-permute-start | bytes 18874376 | tf_op jit(solution)/shard_map/ppermute | solution.py:228
  23.8 21.3 %collective-permute-start.3 = (bf16[192,1024]{1,0:T(8,128)(2,1)S(1)}, bf16[192,1024]{1,0:T(8,128)(2,1)S(1)}, u32[]{:S(2)}, u32[]{:S(2)}) collective-permute-start(bf16[192,1024]{1,0:T(8,128)(2,1)S(1)} %get-tuple-element.69), channel_id=1, source_target_pairs={{0,2},{2,0},{4,6},{6,4},{1,3},{3,1},{5,7},{7,5}} | collective-permute-start | bytes 1179656 | tf_op jit(solution)/shard_map/ppermute | solution.py:202
  26.8 35.2 %collective-permute-start.2 = (bf16[192,1024]{1,0:T(8,128)(2,1)S(1)}, bf16[192,1024]{1,0:T(8,128)(2,1)S(1)}, u32[]{:S(2)}, u32[]{:S(2)}) collective-permute-start(bf16[192,1024]{1,0:T(8,128)(2,1)S(1)} %get-tuple-element.68), channel_id=1, source_target_pairs={{0,2},{2,0},{4,6},{6,4},{1,3},{3,1},{5,7},{7,5}} | collective-permute-start | bytes 1179656 | tf_op jit(solution)/shard_map/ppermute | solution.py:202
  26.8 26.3 %collective-permute-start.4 = (bf16[192,1024]{1,0:T(8,128)(2,1)S(1)}, bf16[192,1024]{1,0:T(8,128)(2,1)S(1)}, u32[]{:S(2)}, u32[]{:S(2)}) collective-permute-start(bf16[192,1024]{1,0:T(8,128)(2,1)S(1)} %get-tuple-element.68), channel_id=1, source_target_pairs={{0,4},{4,0},{2,6},{6,2},{1,5},{5,1},{3,7},{7,3}} | collective-permute-start | bytes 1179656 | tf_op jit(solution)/shard_map/ppermute | solution.py:202
  45.2 20.3 %collective-permute-start.5 = (bf16[192,1024]{1,0:T(8,128)(2,1)S(1)}, bf16[192,1024]{1,0:T(8,128)(2,1)S(1)}, u32[]{:S(2)}, u32[]{:S(2)}) collective-permute-start(bf16[192,1024]{1,0:T(8,128)(2,1)S(1)} %get-tuple-element.69), channel_id=1, source_target_pairs={{0,4},{4,0},{2,6},{6,2},{1,5},{5,1},{3,7},{7,3}} | collective-permute-start | bytes 1179656 | tf_op jit(solution)/shard_map/ppermute | solution.py:202
  53.1 25.6 %collective-permute-start.6 = (bf16[192,1024]{1,0:T(8,128)(2,1)S(1)}, bf16[192,1024]{1,0:T(8,128)(2,1)S(1)}, u32[]{:S(2)}, u32[]{:S(2)}) collective-permute-start(bf16[192,1024]{1,0:T(8,128)(2,1)S(1)} %collective-permute-done.4), channel_id=1, source_target_pairs={{0,2},{2,0},{4,6},{6,4},{1,3},{3,1},{5,7},{7,5}} | collective-permute-start | bytes 1179656 | tf_op jit(solution)/shard_map/ppermute | solution.py:202
  62.0 20.1 %collective-permute-start.7 = (bf16[192,1024]{1,0:T(8,128)(2,1)S(1)}, bf16[192,1024]{1,0:T(8,128)(2,1)S(1)}, u32[]{:S(2)}, u32[]{:S(2)}) collective-permute-start(bf16[192,1024]{1,0:T(8,128)(2,1)S(1)} %collective-permute-done.3), channel_id=1, source_target_pairs={{0,4},{4,0},{2,6},{6,2},{1,5},{5,1},{3,7},{7,3}} | collective-permute-start | bytes 1179656 | tf_op jit(solution)/shard_map/ppermute | solution.py:202
  82.1 15.2 copy-start.4
  89.5 10.0 copy-start.2
  99.5 16.3 copy-start.7
  99.5 20.0 %copy-start.6 = (f32[1024,64]{0,1:T(8,128)S(1)}, f32[1024,64]{0,1:T(8,128)}, u32[]{:S(2)}) copy-start(f32[1024,64]{0,1:T(8,128)} %param.21) | copy-start | bytes 786436
  115.2 370.7 %all-gather.8.cloned.1.call-start = ((), (), s32[]{:S(2)}) async-start(), calls=%async_computation.5 | async-start | bytes 17203200 | tf_op jit(solution)/shard_map/all_gather | solution.py:222
  116.1 73.3 %collective-permute-start.9 = (bf16[192,768]{1,0:T(8,128)(2,1)S(1)}, bf16[192,768]{1,0:T(8,128)(2,1)S(1)}, u32[]{:S(2)}, u32[]{:S(2)}) collective-permute-start(bf16[192,768]{1,0:T(8,128)(2,1)S(1)} %get-tuple-element.71), channel_id=1, source_target_pairs={{0,2},{2,0},{4,6},{6,4},{1,3},{3,1},{5,7},{7,5}} | collective-permute-start | bytes 884744 | tf_op jit(solution)/shard_map/ppermute | solution.py:202
  118.0 69.6 %collective-permute-start.10 = (bf16[192,768]{1,0:T(8,128)(2,1)S(1)}, bf16[192,768]{1,0:T(8,128)(2,1)S(1)}, u32[]{:S(2)}, u32[]{:S(2)}) collective-permute-start(bf16[192,768]{1,0:T(8,128)(2,1)S(1)} %get-tuple-element.70), channel_id=1, source_target_pairs={{0,4},{4,0},{2,6},{6,2},{1,5},{5,1},{3,7},{7,3}} | collective-permute-start | bytes 884744 | tf_op jit(solution)/shard_map/ppermute | solution.py:202
  187.0 40.2 %collective-permute-start.14 = (bf16[4,512,768]{2,1,0:T(8,128)(2,1)}, bf16[4,512,768]{2,1,0:T(8,128)(2,1)}, u32[]{:S(2)}, u32[]{:S(2)}) collective-permute-start(bf16[4,512,768]{2,1,0:T(8,128)(2,1)} %slice_bitcast_fusion.12), channel_id=1, source_target_pairs={{0,1},{1,0},{2,3},{3,2},{4,5},{5,4},{6,7},{7,6}} | collective-permute-start | bytes 9437192 | tf_op jit(solution)/shard_map/ppermute | solution.py:228
  187.0 16.2 collective-permute-start.8
  187.4 16.6 collective-permute-start.11
  187.6 28.1 %collective-permute-start.12 = (bf16[192,768]{1,0:T(8,128)(2,1)S(1)}, bf16[192,768]{1,0:T(8,128)(2,1)S(1)}, u32[]{:S(2)}, u32[]{:S(2)}) collective-permute-start(bf16[192,768]{1,0:T(8,128)(2,1)S(1)} %collective-permute-done.10), channel_id=1, source_target_pairs={{0,2},{2,0},{4,6},{6,4},{1,3},{3,1},{5,7},{7,5}} | collective-permute-start | bytes 884744 | tf_op jit(solution)/shard_map/ppermute | solution.py:202
  189.4 26.6 %collective-permute-start.13 = (bf16[192,768]{1,0:T(8,128)(2,1)S(1)}, bf16[192,768]{1,0:T(8,128)(2,1)S(1)}, u32[]{:S(2)}, u32[]{:S(2)}) collective-permute-start(bf16[192,768]{1,0:T(8,128)(2,1)S(1)} %collective-permute-done.9), channel_id=1, source_target_pairs={{0,4},{4,0},{2,6},{6,2},{1,5},{5,1},{3,7},{7,3}} | collective-permute-start | bytes 884744 | tf_op jit(solution)/shard_map/ppermute | solution.py:202
  216.9 10.2 collective-permute-start.15
  216.9 10.2 slice-start
  216.9 10.3 slice-start.1
  227.1 13.1 copy-start.18
  238.9 0.6 copy-start.16
  239.6 0.6 copy-start.12
  249.1 10.6 collective-permute-start.16
  249.6 962.0 %reduce-scatter.4.cloned.1.call-start = ((), (), s32[]{:S(2)}) async-start(), calls=%async_computation.6 | async-start | bytes 13762560 | tf_op jit(solution)/shard_map/reduce_scatter | solution.py:225
  801.1 38.4 %collective-permute-start.18 = (f32[4,512,1536]{2,1,0:T(8,128)}, f32[4,512,1536]{2,1,0:T(8,128)}, u32[]{:S(2)}, u32[]{:S(2)}) collective-permute-start(f32[4,512,1536]{2,1,0:T(8,128)} %fusion.74), channel_id=1, source_target_pairs={{0,1},{1,0},{2,3},{3,2},{4,5},{5,4},{6,7},{7,6}} | collective-permute-start | bytes 37748744 | tf_op jit(solution)/shard_map/ppermute | solution.py:228
  801.5 38.0 %copy-start.13 = (f32[4,512]{1,0:T(4,128)S(1)}, f32[4,512]{1,0:T(4,128)}, u32[]{:S(2)}) copy-start(f32[4,512]{1,0:T(4,128)} %copy-done.12) | copy-start | bytes 24580
  801.5 38.0 %copy-start.19 = (f32[1536]{0:T(1024)S(1)}, f32[1536]{0:T(1024)}, u32[]{:S(2)}) copy-start(f32[1536]{0:T(1024)} %param.14) | copy-start | bytes 18436
  839.4 41.4 %copy-start.17 = (f32[4,512]{1,0:T(4,128)S(1)}, f32[4,512]{1,0:T(4,128)}, u32[]{:S(2)}) copy-start(f32[4,512]{1,0:T(4,128)} %copy-done.16) | copy-start | bytes 24580
  891.4 2.7 copy-start
  894.1 10.2 collective-permute-start.19
  904.3 19.0 %slice-start.4 = ((s8[6291456]{0:T(1024)(128)(4,1)}), s8[4194304]{0:T(1024)(128)(4,1)S(1)}, s32[]{:S(2)}) async-start(s8[6291456]{0:T(1024)(128)(4,1)} %bitcast.170), calls=%async_computation.13 | async-start | bytes 8388608
  907.8 15.5 copy-start.1
  907.8 15.5 slice-start.5
  1062.8 563.3 %reduce-scatter.6.cloned.1.call-start = ((), (), s32[]{:S(2)}) async-start(), calls=%async_computation.7 | async-start | bytes 68812800 | tf_op jit(solution)/shard_map/reduce_scatter | solution.py:225
  1063.4 801.4 %reduce-scatter.8.cloned.1.call-start = ((), (), s32[]{:S(2)}) async-start(), calls=%async_computation.8 | async-start | bytes 34406400 | tf_op jit(solution)/shard_map/reduce_scatter | solution.py:225
  1063.9 39.6 %copy-start.5 = (bf16[1536,1024]{1,0:T(8,128)(2,1)S(1)}, bf16[1536,1024]{1,0:T(8,128)(2,1)}, u32[]{:S(2)}) copy-start(bf16[1536,1024]{1,0:T(8,128)(2,1)} %copy-done.4) | copy-start | bytes 9437188
  1103.4 19.5 %collective-permute-start.17 = (f32[4,512,1536]{2,1,0:T(8,128)}, f32[4,512,1536]{2,1,0:T(8,128)}, u32[]{:S(2)}, u32[]{:S(2)}) collective-permute-start(f32[4,512,1536]{2,1,0:T(8,128)} %fusion.18), channel_id=1, source_target_pairs={{0,1},{1,0},{2,3},{3,2},{4,5},{5,4},{6,7},{7,6}} | collective-permute-start | bytes 37748744 | tf_op jit(solution)/shard_map/ppermute | solution.py:228
  1103.5 58.4 %slice-start.2 = ((s8[6291456]{0:T(1024)(128)(4,1)}), s8[4194304]{0:T(1024)(128)(4,1)S(1)}, s32[]{:S(2)}) async-start(s8[6291456]{0:T(1024)(128)(4,1)} %bitcast.165), calls=%async_computation.11 | async-start | bytes 8388608
  1115.4 46.5 %slice-start.3 = ((s8[6291456]{0:T(1024)(128)(4,1)}), s8[2097152]{0:T(1024)(128)(4,1)S(1)}, s32[]{:S(2)}) async-start(s8[6291456]{0:T(1024)(128)(4,1)} %bitcast.165), calls=%async_computation.12 | async-start | bytes 4194304
  1115.4 46.6 %copy-start.9 = (f32[4,512]{1,0:T(4,128)S(1)}, f32[4,512]{1,0:T(4,128)}, u32[]{:S(2)}) copy-start(f32[4,512]{1,0:T(4,128)} %copy-done.8) | copy-start | bytes 24580
  1115.4 46.6 %copy-start.15 = (f32[1536]{0:T(1024)S(1)}, f32[1536]{0:T(1024)}, u32[]{:S(2)}) copy-start(f32[1536]{0:T(1024)} %param.13) | copy-start | bytes 18436
  1115.4 46.5 %collective-permute-start.20 = (f32[4,512,1536]{2,1,0:T(8,128)}, f32[4,512,1536]{2,1,0:T(8,128)}, u32[]{:S(2)}, u32[]{:S(2)}) collective-permute-start(f32[4,512,1536]{2,1,0:T(8,128)} %fusion.86), channel_id=1, source_target_pairs={{0,1},{1,0},{2,3},{3,2},{4,5},{5,4},{6,7},{7,6}} | collective-permute-start | bytes 37748744 | tf_op jit(solution)/shard_map/ppermute | solution.py:228
  1161.9 15.3 copy-start.20
  1161.9 39.0 %copy-start.11 = (f32[4,512]{1,0:T(4,128)S(1)}, f32[4,512]{1,0:T(4,128)}, u32[]{:S(2)}) copy-start(f32[4,512]{1,0:T(4,128)} %copy-done.10) | copy-start | bytes 24580
Sparse Core Ops, SparseCore 0:
  9.8 161.0 all-gather.3
  172.6 139.2 all-gather.5
  313.7 126.5 all-gather.7
  1062.9 102.3 reduce-scatter.3
  1168.2 457.8 reduce-scatter.5
  1629.5 235.2 reduce-scatter.7
